TPU v7x, 128 devices: a whole 4x4x4 slice. The times are simulated.
128 devices in a mesh: rows: 32 (over y, x, core), cols: 4 (over z).
Axes of the slice: x: 4, y: 4, z: 4, core: 2. Of those that a mesh axis runs over, the one named last changes fastest.
Arguments:
- terminal_value: float32 [4096, 2048], P('rows', 'cols'), may hold values from -6 to 6
- density_start: float32 [4096, 2048], P('rows', 'cols'), may hold values from 0.2 to 3
- start_cells: int32 [524288], P(('rows', 'cols')), may hold values from 0 to 65535
- offsets: float32 [2, 524288], P(None, ('rows', 'cols')), may hold values from -4 to 4
- weights: float32 [524288], P(('rows', 'cols')), may hold values from 0.3 to 9
- dest_tiles: int32 [4096], P(('rows', 'cols')), may hold values from 0 to 127, as said below
- end_cells: int32 [524288], P(('rows', 'cols')), may hold values from 0 to 65535
Outputs:
- value: float32 [4096, 2048], P('rows', 'cols')
- density: float32 [4096, 2048], P('rows', 'cols')
Inputs may be any that keep to these rules, and one draw needn't show every extreme that they name: `dest_tiles`: block b's tile lies in the band of the tile where b starts or in a band next to it. At most 8 blocks that start in one tile go to any one tile, and for every starting tile there is one destination tile that receives exactly 8 of its blocks.
All inputs are finite; a program needn't handle non-finite values.
Results may differ from a plain program's by a relative error of at most 0.0003.
Values sent between devices are 32-bit elements; how exact they have to be, the bound alone decides.
A program may use at most 64 MiB of HBM per device.

v0:
```python
import jax
import jax.numpy as jnp
from jax import lax
from jax.sharding import Mesh
from jax.sharding import PartitionSpec as P

HJB_STEPS = 4
ITERS = 2
ROWS_COLS = ("rows_0", "rows_1", "rows_2", "cols")
ROWS = ("rows_0", "rows_1", "rows_2")


def padded_2(value, sides, width):
    for axis, dim in sides:
        peers, length = (lax.axis_size(axis), value.shape[dim])
        up = [(i, (i + 1) % peers) for i in range(peers - 1)]
        down = [(j, i) for i, j in up]
        last = lax.slice_in_dim(value, length - width, length, axis=dim)
        initial = lax.slice_in_dim(value, 0, width, axis=dim)
        before = lax.ppermute(last, axis, up)
        after = lax.ppermute(initial, axis, down)
        value = jnp.concatenate([before, value, after], axis=dim)
    return value


def from_behind(value, axis, steps):
    count = lax.axis_size(axis)
    initial, last = (max(0, -steps), min(count, count - steps))
    return lax.ppermute(value, axis, [(source, source + steps) for source in range(initial, last)])


def one_axis_at_a_time(value, axes):
    for axis in axes:
        value = lax.psum(value, axis)
    return value


def hjb_update(padded, density):
    value = padded[1:-1, 1:-1]
    up = padded[:-2, 1:-1]
    down = padded[2:, 1:-1]
    left = padded[1:-1, :-2]
    right = padded[1:-1, 2:]
    back_x = jnp.maximum(value - up, 0.0)
    fore_x = jnp.minimum(down - value, 0.0)
    back_y = jnp.maximum(value - left, 0.0)
    fore_y = jnp.minimum(right - value, 0.0)
    square_x = jnp.maximum(back_x * back_x, fore_x * fore_x)
    square_y = jnp.maximum(back_y * back_y, fore_y * fore_y)
    spread = up + down + left + right - 4.0 * value
    return value + 0.25 * (0.5 * spread - 0.5 * (square_x + square_y) + 0.5 * density)


def sweep_once(deep_value, density, inside):
    widened = padded_2(density, ((ROWS, 0), ("cols", 1)), HJB_STEPS)
    current = deep_value
    for inner in range(HJB_STEPS):
        local_density = widened[inner : widened.shape[0] - inner, inner : widened.shape[1] - inner]
        trim = inner + 1
        kept = inside[trim : inside.shape[0] - trim, trim : inside.shape[1] - trim]
        updated = hjb_update(current, local_density)
        current = jnp.where(kept, updated, 0.0)
    return current


def group_size(count, unit, most):
    group = unit
    while count % (group * 2) == 0 and group * 2 <= most:
        group = group * 2
    return group


def route_cells(buffer, n_cols, cap):
    sectioned = buffer.reshape((3, n_cols * cap) + buffer.shape[1:])
    pieces = [sectioned[1]]
    for section, step in ((0, -1), (2, 1)):
        pieces.append(from_behind(sectioned[section], ROWS, step))
    gathered = jnp.stack(pieces, axis=0)
    gathered = lax.all_to_all(gathered, "cols", split_axis=1, concat_axis=1, tiled=True)
    return gathered.reshape((3 * n_cols * cap,) + buffer.shape[1:])


def route_moves(buffer, n_cols, cap):
    sectioned = buffer.reshape((3, n_cols * cap) + buffer.shape[1:])
    pieces = [sectioned[1]]
    for section, step in ((0, -1), (2, 1)):
        pieces.append(from_behind(sectioned[section], ROWS, step))
    gathered = jnp.stack(pieces, axis=0)
    gathered = lax.all_to_all(gathered, "cols", split_axis=1, concat_axis=1, tiled=True)
    return gathered.reshape((3 * n_cols * cap,) + buffer.shape[1:])


def sample_corners(padded, start_cells, cols_here, block_len):
    rows_pad, cols_pad = padded.shape
    count = start_cells.shape[0]
    group = group_size(count, block_len, 512)
    row_top = (start_cells // cols_here + 1).reshape(-1, group)
    col_left = (start_cells % cols_here + 1).reshape(-1, group)
    row_iota = jnp.arange(rows_pad, dtype=jnp.int32)
    col_iota = jnp.arange(cols_pad, dtype=jnp.int32)

    def step(carry, item):
        top, left = item
        upper_pick = (top[:, None] == row_iota[None, :]).astype(jnp.float32)
        lower_pick = (top[:, None] + 1 == row_iota[None, :]).astype(jnp.float32)
        picks = jnp.concatenate([upper_pick, lower_pick], axis=0)
        lines = jnp.dot(
            picks, padded, precision=lax.Precision.HIGHEST, preferred_element_type=jnp.float32
        )
        upper = lines[:group]
        lower = lines[group:]
        left_mask = left[:, None] == col_iota[None, :]
        right_mask = left[:, None] + 1 == col_iota[None, :]
        corner_a = jnp.sum(jnp.where(left_mask, upper, 0.0), axis=1)
        corner_b = jnp.sum(jnp.where(left_mask, lower, 0.0), axis=1)
        corner_c = jnp.sum(jnp.where(right_mask, upper, 0.0), axis=1)
        corner_d = jnp.sum(jnp.where(right_mask, lower, 0.0), axis=1)
        return (carry, jnp.stack([corner_a, corner_b, corner_c, corner_d], axis=0))

    unused, corners = lax.scan(step, jnp.zeros((), jnp.float32), (row_top, col_left))
    corners = jnp.transpose(corners, (1, 0, 2)).reshape(4, count)
    return (corners[0], corners[1], corners[2], corners[3])


def deposit_mass(arrived, arrived_cells, rows_here, cols_here, n_rows, n_cols):
    block_len = arrived.shape[2]
    move_x = arrived[:, 0].reshape(-1)
    move_y = arrived[:, 1].reshape(-1)
    masses = arrived[:, 2].reshape(-1)
    cells = arrived_cells.reshape(-1)
    count = cells.shape[0]
    group = group_size(count, block_len, 512)
    row_iota = jnp.arange(rows_here + 1, dtype=jnp.int32)
    col_iota = jnp.arange(cols_here + 1, dtype=jnp.int32)

    def step(total, item):
        part_x, part_y, part_mass, part_cells = item
        row_cell = part_cells // cols_here
        col_cell = part_cells % cols_here
        row_side = jnp.where(
            row_iota[None, :] == row_cell[:, None],
            part_mass[:, None] * (1.0 - part_x[:, None]),
            0.0,
        )
        row_side = row_side + jnp.where(
            row_iota[None, :] == row_cell[:, None] + 1, part_mass[:, None] * part_x[:, None], 0.0
        )
        col_side = jnp.where(col_iota[None, :] == col_cell[:, None], 1.0 - part_y[:, None], 0.0)
        col_side = col_side + jnp.where(
            col_iota[None, :] == col_cell[:, None] + 1, part_y[:, None], 0.0
        )
        added = lax.dot_general(
            row_side,
            col_side,
            (((0,), (0,)), ((), ())),
            precision=lax.Precision.HIGHEST,
            preferred_element_type=jnp.float32,
        )
        return (total + added, None)

    items = (
        move_x.reshape(-1, group),
        move_y.reshape(-1, group),
        masses.reshape(-1, group),
        cells.reshape(-1, group),
    )
    grid, unused = lax.scan(step, jnp.zeros((rows_here + 1, cols_here + 1), jnp.float32), items)
    last_band = lax.axis_index(ROWS) == n_rows - 1
    last_column = lax.axis_index("cols") == n_cols - 1
    spill_row = grid[rows_here]
    below = from_behind(spill_row, ROWS, 1)
    upper = grid[:rows_here].at[0].add(below)
    upper = upper.at[rows_here - 1].add(jnp.where(last_band, spill_row, 0.0))
    spill_col = upper[:, cols_here]
    beside = from_behind(spill_col, "cols", 1)
    placed = upper[:, :cols_here].at[:, 0].add(beside)
    return placed.at[:, cols_here - 1].add(jnp.where(last_column, spill_col, 0.0))


def body(terminal_value, density_start, start_cells, offsets, weights, dest_tiles, end_cells):
    rows_here, cols_here = terminal_value.shape
    n_rows = lax.axis_size(ROWS)
    n_cols = lax.axis_size("cols")
    blocks = dest_tiles.shape[0]
    block_len = weights.shape[0] // blocks
    cap = blocks // 4
    frac_x = 0.5 + 0.45 * jnp.tanh(offsets[0])
    frac_y = 0.5 + 0.45 * jnp.tanh(offsets[1])
    same = dest_tiles[:, None] == dest_tiles[None, :]
    counter = jnp.arange(blocks, dtype=jnp.int32)
    earlier = counter[:, None] > counter[None, :]
    rank = jnp.sum(same & earlier, axis=1)
    my_band = lax.axis_index(ROWS)
    slots = ((dest_tiles // n_cols - my_band + 1) * n_cols + dest_tiles % n_cols) * cap + rank
    slot_count = 3 * n_cols * cap
    slot_iota = jnp.arange(slot_count, dtype=jnp.int32)
    placing = slot_iota[:, None] == slots[None, :]
    placing_float = placing.astype(jnp.float32)
    cell_blocks = end_cells.reshape(blocks, block_len)
    cell_buffer = jnp.sum(jnp.where(placing[:, :, None], cell_blocks[None, :, :], 0), axis=1)
    arrived_cells = route_cells(cell_buffer, n_cols, cap)
    total_cells = rows_here * cols_here * n_rows * n_cols
    total = one_axis_at_a_time(jnp.sum(weights), ROWS_COLS)
    scale = total_cells / total
    depth = HJB_STEPS + 1
    deep_value = padded_2(terminal_value, ((ROWS, 0), ("cols", 1)), depth)
    global_rows = (
        lax.axis_index(ROWS) * rows_here
        - depth
        + jnp.arange(rows_here + 2 * depth, dtype=jnp.int32)
    )
    global_cols = (
        lax.axis_index("cols") * cols_here
        - depth
        + jnp.arange(cols_here + 2 * depth, dtype=jnp.int32)
    )
    inside_rows = (global_rows >= 0) & (global_rows < rows_here * n_rows)
    inside_cols = (global_cols >= 0) & (global_cols < cols_here * n_cols)
    inside = inside_rows[:, None] & inside_cols[None, :]
    density = density_start
    value = terminal_value
    for outer in range(ITERS):
        padded = sweep_once(deep_value, density, inside)
        value = padded[1:-1, 1:-1]
        corner_a, corner_b, corner_c, corner_d = sample_corners(
            padded, start_cells, cols_here, block_len
        )
        grad_x = (1.0 - frac_y) * (corner_b - corner_a) + frac_y * (corner_d - corner_c)
        grad_y = (1.0 - frac_x) * (corner_c - corner_a) + frac_x * (corner_d - corner_b)
        moved_x = 0.5 + 0.45 * jnp.tanh(offsets[0] - grad_x)
        moved_y = 0.5 + 0.45 * jnp.tanh(offsets[1] - grad_y)
        payload = jnp.stack(
            [
                moved_x.reshape(blocks, block_len),
                moved_y.reshape(blocks, block_len),
                weights.reshape(blocks, block_len),
            ],
            axis=1,
        )
        move_buffer = jnp.einsum(
            "sb,bkl->skl", placing_float, payload, precision=lax.Precision.HIGHEST
        )
        arrived = route_moves(move_buffer, n_cols, cap)
        deposit = deposit_mass(arrived, arrived_cells, rows_here, cols_here, n_rows, n_cols)
        fresh = deposit * scale
        density = 0.5 * density + 0.5 * fresh
    return (value, density)


def solution(mesh):
    split = Mesh(
        mesh.devices.reshape(4, 4, 2, mesh.shape["cols"]), ("rows_0", "rows_1", "rows_2", "cols")
    )
    return jax.shard_map(
        body,
        mesh=split,
        in_specs=(
            P(ROWS, "cols"),
            P(ROWS, "cols"),
            P(ROWS_COLS),
            P(None, ROWS_COLS),
            P(ROWS_COLS),
            P(ROWS_COLS),
            P(ROWS_COLS),
        ),
        out_specs=(P(ROWS, "cols"), P(ROWS, "cols")),
        check_vma=False,
    )
```

profile of v0, /device:TPU:40, one launch (start us, length us, event | category | flops | bytes accessed | tf_op | source)
XLA Modules:
  0.0 304.9 jit_solution(1589758791255645497)
XLA Ops:
  1.6 1.9 collective-permute-start
  3.7 5.8 %collective-permute-start.1 = (f32[5,512]{0,1:T(8,128)S(1)}, f32[5,512]{0,1:T(8,128)S(1)}, u32[]{:S(2)}, u32[]{:S(2)}) collective-permute-start(f32[5,512]{0,1:T(8,128)S(1)} %copy.125), channel_id=1, source_target_pairs={{4,0},{8,4},{12,8},{16,12},{20,16},{24,20},{28,24},{32,28},{36,32}... | collective-permute-start | bytes 30728 | tf_op jit(solution)/shard_map/ppermute | solution.py:21
  10.4 1.9 collective-permute-start.6
  12.4 5.8 %collective-permute-start.7 = (f32[4,512]{0,1:T(8,128)S(1)}, f32[4,512]{0,1:T(8,128)S(1)}, u32[]{:S(2)}, u32[]{:S(2)}) collective-permute-start(f32[4,512]{0,1:T(8,128)S(1)} %copy.131), channel_id=1, source_target_pairs={{4,0},{8,4},{12,8},{16,12},{20,16},{24,20},{28,24},{32,28},{36,32}... | collective-permute-start | bytes 24584 | tf_op jit(solution)/shard_map/ppermute | solution.py:21
  21.3 1.9 collective-permute-start.4
  23.9 2.4 collective-permute-start.5
  26.4 3.8 %collective-permute-start.2 = (f32[138,5]{0,1:T(8,128)S(1)}, f32[138,5]{0,1:T(8,128)S(1)}, u32[]{:S(2)}, u32[]{:S(2)}) collective-permute-start(f32[138,5]{0,1:T(8,128)S(1)} %get-tuple-element.733), channel_id=1, source_target_pairs={{0,1},{1,2},{2,3},{4,5},{5,6},{6,7},{8,9},{9,10},{10,11},{12,13},{... | collective-permute-start | bytes 8288 | tf_op jit(solution)/shard_map/ppermute | solution.py:20
  30.2 2.0 collective-permute-start.3
  32.3 3.8 %collective-permute-start.8 = (f32[136,4]{0,1:T(4,128)S(1)}, f32[136,4]{0,1:T(4,128)S(1)}, u32[]{:S(2)}, u32[]{:S(2)}) collective-permute-start(f32[136,4]{0,1:T(4,128)S(1)} %get-tuple-element.731), channel_id=1, source_target_pairs={{0,1},{1,2},{2,3},{4,5},{5,6},{6,7},{8,9},{9,10},{10,11},{12,13},{... | collective-permute-start | bytes 6536 | tf_op jit(solution)/shard_map/ppermute | solution.py:20
  36.1 2.0 collective-permute-start.9
  38.5 3.2 %collective-permute-done.9 = f32[136,4]{0,1:T(4,128)S(1)} collective-permute-done((f32[136,4]{0,1:T(4,128)S(1)}, f32[136,4]{0,1:T(4,128)S(1)}, u32[]{:S(2)}, u32[]{:S(2)}) %collective-permute-start.9) | collective-permute-done | bytes 2208 | tf_op jit(solution)/shard_map/ppermute | solution.py:21
  45.8 15.0 %while.60 = (s32[]{:T(128)}, f32[8,4,512]{2,1,0:T(4,128)S(1)}, s32[8,512]{1,0:T(8,128)S(1)}, s32[8,512]{1,0:T(8,128)S(1)}, f32[130,514]{1,0:T(8,128)S(1)}, /*index=5*/s32[]{:T(128)}) while((s32[]{:T(128)}, f32[8,4,512]{2,1,0:T(4,128)S(1)}, s32[8,512]{1,0:T(8,128)S(1)}, s32[8,512]{1,0:T(8,128)S(1)}, ...), condition=%wide.region_6.7_spmd.clone.clone, body=%wide.region_1.6_spmd.clone.clone.sunk | while | flops 823987200 | bytes 4793437 | solution.py:120
  61.3 3.3 %collective-permute-start.10 = (f32[32,3,128]{2,0,1:T(8,128)S(1)}, f32[32,3,128]{2,0,1:T(8,128)S(1)}, u32[]{:S(2)}, u32[]{:S(2)}) collective-permute-start(f32[32,3,128]{2,0,1:T(8,128)S(1)} %get-tuple-element.752), channel_id=1, source_target_pairs={{4,0},{8,4},{12,8},{16,12},{20,16},{24,20},{28,24},{32,28},{36,32}... | collective-permute-start | bytes 147464 | tf_op jit(solution)/shard_map/ppermute | solution.py:29
  64.6 1.9 collective-permute-start.11
  67.3 5.0 %all-to-all-start = ((s32[3,32,128]{2,0,1:T(4,128)}), s32[3,32,128]{2,0,1:T(4,128)S(1)}, u32[]{:S(2)}, u32[]{:S(2)}) async-start(s32[3,32,128]{2,0,1:T(4,128)} %copy.128), calls=%async_computation | async-start | bytes 131072 | tf_op jit(solution)/shard_map/all_to_all | solution.py:79
  73.0 3.4 %all-to-all-done = s32[3,32,128]{2,0,1:T(4,128)S(1)} async-done(((s32[3,32,128]{2,0,1:T(4,128)}), s32[3,32,128]{2,0,1:T(4,128)S(1)}, u32[]{:S(2)}, u32[]{:S(2)}) %all-to-all-start) | async-done | bytes 49184 | tf_op jit(solution)/shard_map/all_to_all | solution.py:79
  76.4 4.8 %all-to-all-start.1 = ((f32[3,32,3,128]{3,2,0,1:T(4,128)}), f32[3,32,3,128]{3,2,0,1:T(4,128)S(1)}, u32[]{:S(2)}, u32[]{:S(2)}) async-start(f32[3,32,3,128]{3,2,0,1:T(4,128)} %copy.134), calls=%async_computation.1 | async-start | bytes 393216 | tf_op jit(solution)/shard_map/all_to_all | solution.py:89
  81.2 4.9 %all-to-all-done.1 = f32[3,32,3,128]{3,2,0,1:T(4,128)S(1)} async-done(((f32[3,32,3,128]{3,2,0,1:T(4,128)}), f32[3,32,3,128]{3,2,0,1:T(4,128)S(1)}, u32[]{:S(2)}, u32[]{:S(2)}) %all-to-all-start.1) | async-done | bytes 147488 | tf_op jit(solution)/shard_map/all_to_all | solution.py:89
  86.1 47.6 %while.62 = (s32[]{:T(128)}, f32[129,513]{1,0:T(8,128)S(1)}, s32[24,512]{1,0:T(8,128)S(1)}, f32[24,512]{1,0:T(8,128)S(1)}, f32[24,512]{1,0:T(8,128)S(1)}, /*index=5*/f32[24,512]{1,0:T(8,128)S(1)}, s32[]{:T(128)}, s32[]{:T(128)}) while((s32[]{:T(128)}, f32[129,513]{1,0:T(8,128)S(1)}, s32[24,512]{1,0:T(8,128)S(1)}, ...), condition=%wide.region_9.10_spmd.clone.clone, body=%wide.region_8.9_spmd.clone.clone.sunk | while | flops 408380160 | bytes 584819 | solution.py:167
  88.2 1.9 fusion.193
  94.2 1.9 fusion.193
  100.1 1.9 fusion.193
  106.1 1.9 fusion.193
  110.1 1.9 fusion.193
  134.1 1.9 collective-permute-start.12
  136.7 9.5 %psum.28 = f32[]{:T(128)} all-reduce(f32[]{:T(128)} %reduce_sum.101), channel_id=1, replica_groups=mesh['rows_0'=4,'rows_1'=4,'rows_2'=2,'cols'=4] {'rows_0'}, use_global_device_ids=true, to_apply=%region_12.13 | all-reduce | flops 1 | bytes 8 | tf_op jit(solution)/shard_map/psum | solution.py:34
  148.1 2.0 scatter-add.29
  150.1 1.9 collective-permute-start.13
  152.0 9.8 %psum.29 = f32[]{:T(128)} all-reduce(f32[]{:T(128)} %psum.28), channel_id=1, replica_groups=mesh['rows_0'=4,'rows_1'=4,'rows_2'=2,'cols'=4] {'rows_1'}, use_global_device_ids=true, to_apply=%region_13.14 | all-reduce | flops 1 | bytes 8 | tf_op jit(solution)/shard_map/psum | solution.py:34
  161.8 3.1 %psum.30 = f32[]{:T(128)} all-reduce(f32[]{:T(128)} %psum.29), channel_id=1, replica_groups=mesh['rows_0'=4,'rows_1'=4,'rows_2'=2,'cols'=4] {'rows_2'}, use_global_device_ids=true, to_apply=%region_14.15 | all-reduce | flops 1 | bytes 8 | tf_op jit(solution)/shard_map/psum | solution.py:34
  164.9 10.3 %psum.31 = f32[]{:T(128)} all-reduce(f32[]{:T(128)} %psum.30), channel_id=1, replica_groups=mesh['rows_0'=4,'rows_1'=4,'rows_2'=2,'cols'=4] {'cols'}, use_global_device_ids=true, to_apply=%region_15.16 | all-reduce | flops 1 | bytes 8 | tf_op jit(solution)/shard_map/psum | solution.py:34
  177.5 1.9 collective-permute-start.14
  179.5 5.8 %collective-permute-start.15 = (f32[4,512]{0,1:T(8,128)S(1)}, f32[4,512]{0,1:T(8,128)S(1)}, u32[]{:S(2)}, u32[]{:S(2)}) collective-permute-start(f32[4,512]{0,1:T(8,128)S(1)} %get-tuple-element.736), channel_id=1, source_target_pairs={{4,0},{8,4},{12,8},{16,12},{20,16},{24,20},{28,24},{32,28},{36,32}... | collective-permute-start | bytes 24584 | tf_op jit(solution)/shard_map/ppermute | solution.py:21
  185.2 2.1 collective-permute-done.14
  189.2 1.9 collective-permute-start.16
  191.1 3.9 %collective-permute-start.17 = (f32[136,4]{0,1:T(4,128)S(1)}, f32[136,4]{0,1:T(4,128)S(1)}, u32[]{:S(2)}, u32[]{:S(2)}) collective-permute-start(f32[136,4]{0,1:T(4,128)S(1)} %get-tuple-element.730), channel_id=1, source_target_pairs={{1,0},{2,1},{3,2},{5,4},{6,5},{7,6},{9,8},{10,9},{11,10},{13,12},{... | collective-permute-start | bytes 6536 | tf_op jit(solution)/shard_map/ppermute | solution.py:21
  200.3 15.0 %while.61 = (s32[]{:T(128)}, f32[8,4,512]{2,1,0:T(4,128)S(1)}, s32[8,512]{1,0:T(8,128)S(1)}, s32[8,512]{1,0:T(8,128)S(1)}, f32[130,514]{1,0:T(8,128)S(1)}, /*index=5*/s32[]{:T(128)}) while((s32[]{:T(128)}, f32[8,4,512]{2,1,0:T(4,128)S(1)}, s32[8,512]{1,0:T(8,128)S(1)}, s32[8,512]{1,0:T(8,128)S(1)}, ...), condition=%wide.region_21.22_spmd.clone.clone, body=%wide.region_16.21_spmd.clone.clone.sunk | while | flops 823987200 | bytes 4793437 | solution.py:120
  215.8 4.8 %collective-permute-start.18 = (f32[32,3,128]{2,0,1:T(8,128)S(1)}, f32[32,3,128]{2,0,1:T(8,128)S(1)}, u32[]{:S(2)}, u32[]{:S(2)}) collective-permute-start(f32[32,3,128]{2,0,1:T(8,128)S(1)} %get-tuple-element.746), channel_id=1, source_target_pairs={{4,0},{8,4},{12,8},{16,12},{20,16},{24,20},{28,24},{32,28},{36,32}... | collective-permute-start | bytes 147464 | tf_op jit(solution)/shard_map/ppermute | solution.py:29
  220.5 1.9 collective-permute-start.19
  222.5 5.6 %collective-permute-done.19 = f32[32,3,128]{2,0,1:T(8,128)S(1)} collective-permute-done((f32[32,3,128]{2,0,1:T(8,128)S(1)}, f32[32,3,128]{2,0,1:T(8,128)S(1)}, u32[]{:S(2)}, u32[]{:S(2)}) %collective-permute-start.19) | collective-permute-done | bytes 49184 | tf_op jit(solution)/shard_map/ppermute | solution.py:29
  228.9 5.1 %all-to-all-start.2 = ((f32[3,32,3,128]{3,2,0,1:T(4,128)}), f32[3,32,3,128]{3,2,0,1:T(4,128)S(1)}, u32[]{:S(2)}, u32[]{:S(2)}) async-start(f32[3,32,3,128]{3,2,0,1:T(4,128)} %copy.141), calls=%async_computation.2 | async-start | bytes 393216 | tf_op jit(solution)/shard_map/all_to_all | solution.py:89
  233.9 4.9 %all-to-all-done.2 = f32[3,32,3,128]{3,2,0,1:T(4,128)S(1)} async-done(((f32[3,32,3,128]{3,2,0,1:T(4,128)}), f32[3,32,3,128]{3,2,0,1:T(4,128)S(1)}, u32[]{:S(2)}, u32[]{:S(2)}) %all-to-all-start.2) | async-done | bytes 147488 | tf_op jit(solution)/shard_map/all_to_all | solution.py:89
  238.9 47.6 %while.63 = (s32[]{:T(128)}, f32[129,513]{1,0:T(8,128)S(1)}, s32[24,512]{1,0:T(8,128)S(1)}, f32[24,512]{1,0:T(8,128)S(1)}, f32[24,512]{1,0:T(8,128)S(1)}, /*index=5*/f32[24,512]{1,0:T(8,128)S(1)}, s32[]{:T(128)}, s32[]{:T(128)}) while((s32[]{:T(128)}, f32[129,513]{1,0:T(8,128)S(1)}, s32[24,512]{1,0:T(8,128)S(1)}, ...), condition=%wide.region_23.24_spmd.clone.clone, body=%wide.region_22.23_spmd.clone.clone.sunk | while | flops 408380160 | bytes 584819 | solution.py:167
  286.9 1.9 collective-permute-start.20
  288.9 5.1 %collective-permute-done.20 = f32[513]{0:T(1024)S(1)} collective-permute-done((f32[513]{0:T(1024)S(1)}, f32[513]{0:T(1024)S(1)}, u32[]{:S(2)}, u32[]{:S(2)}) %collective-permute-start.20) | collective-permute-done | bytes 2084 | tf_op jit(solution)/shard_map/ppermute | solution.py:29
  295.8 2.0 scatter-add.35
  297.8 1.9 collective-permute-start.21
  300.8 2.5 collective-permute-done.21
  (585 shorter events, 141.5 us)
Async XLA Ops:
  0.6 22.9 %copy-start = (f32[128,512]{1,0:T(8,128)S(1)}, f32[128,512]{1,0:T(8,128)}, u32[]{:S(2)}) copy-start(f32[128,512]{1,0:T(8,128)} %param.31) | copy-start | bytes 786436
  0.6 23.0 %copy-start.1 = (f32[128,512]{1,0:T(8,128)S(1)}, f32[128,512]{1,0:T(8,128)}, u32[]{:S(2)}) copy-start(f32[128,512]{1,0:T(8,128)} %param.32) | copy-start | bytes 786436
  0.7 22.7 %copy-start.3 = (f32[2,4096]{1,0:T(2,128)S(1)}, f32[2,4096]{1,0:T(2,128)}, u32[]{:S(2)}) copy-start(f32[2,4096]{1,0:T(2,128)} %param.34) | copy-start | bytes 98308
  0.7 22.8 %copy-start.4 = (s32[4096]{0:T(1024)S(1)}, s32[4096]{0:T(1024)}, u32[]{:S(2)}) copy-start(s32[4096]{0:T(1024)} %param.33) | copy-start | bytes 49156
  1.6 22.2 %collective-permute-start = (f32[5,512]{0,1:T(8,128)S(1)}, f32[5,512]{0,1:T(8,128)S(1)}, u32[]{:S(2)}, u32[]{:S(2)}) collective-permute-start(f32[5,512]{0,1:T(8,128)S(1)} %copy.124), channel_id=1, source_target_pairs={{0,4},{4,8},{8,12},{12,16},{16,20},{20,24},{24,28},{28,32},{32,36}... | collective-permute-start | bytes 30728 | tf_op jit(solution)/shard_map/ppermute | solution.py:20
  3.7 22.6 %collective-permute-start.1 = (f32[5,512]{0,1:T(8,128)S(1)}, f32[5,512]{0,1:T(8,128)S(1)}, u32[]{:S(2)}, u32[]{:S(2)}) collective-permute-start(f32[5,512]{0,1:T(8,128)S(1)} %copy.125), channel_id=1, source_target_pairs={{4,0},{8,4},{12,8},{16,12},{20,16},{24,20},{28,24},{32,28},{36,32}... | collective-permute-start | bytes 30728 | tf_op jit(solution)/shard_map/ppermute | solution.py:21
  10.4 19.8 %collective-permute-start.6 = (f32[4,512]{0,1:T(8,128)S(1)}, f32[4,512]{0,1:T(8,128)S(1)}, u32[]{:S(2)}, u32[]{:S(2)}) collective-permute-start(f32[4,512]{0,1:T(8,128)S(1)} %copy.130), channel_id=1, source_target_pairs={{0,4},{4,8},{8,12},{12,16},{16,20},{20,24},{24,28},{28,32},{32,36}... | collective-permute-start | bytes 24584 | tf_op jit(solution)/shard_map/ppermute | solution.py:20
  12.4 19.8 %collective-permute-start.7 = (f32[4,512]{0,1:T(8,128)S(1)}, f32[4,512]{0,1:T(8,128)S(1)}, u32[]{:S(2)}, u32[]{:S(2)}) collective-permute-start(f32[4,512]{0,1:T(8,128)S(1)} %copy.131), channel_id=1, source_target_pairs={{4,0},{8,4},{12,8},{16,12},{20,16},{24,20},{28,24},{32,28},{36,32}... | collective-permute-start | bytes 24584 | tf_op jit(solution)/shard_map/ppermute | solution.py:21
  21.3 45.2 %collective-permute-start.4 = (s32[32,128]{1,0:T(8,128)S(1)}, s32[32,128]{1,0:T(8,128)S(1)}, u32[]{:S(2)}, u32[]{:S(2)}) collective-permute-start(s32[32,128]{1,0:T(8,128)S(1)} %get-tuple-element.763), channel_id=1, source_target_pairs={{4,0},{8,4},{12,8},{16,12},{20,16},{24,20},{28,24},{32,28},{36,32}... | collective-permute-start | bytes 49160 | tf_op jit(solution)/shard_map/ppermute | solution.py:29
  23.9 42.7 %collective-permute-start.5 = (s32[32,128]{1,0:T(8,128)S(1)}, s32[32,128]{1,0:T(8,128)S(1)}, u32[]{:S(2)}, u32[]{:S(2)}) collective-permute-start(s32[32,128]{1,0:T(8,128)S(1)} %get-tuple-element.762), channel_id=1, source_target_pairs={{0,4},{4,8},{8,12},{12,16},{16,20},{20,24},{24,28},{28,32},{32,36}... | collective-permute-start | bytes 49160 | tf_op jit(solution)/shard_map/ppermute | solution.py:29
  26.4 9.8 %collective-permute-start.2 = (f32[138,5]{0,1:T(8,128)S(1)}, f32[138,5]{0,1:T(8,128)S(1)}, u32[]{:S(2)}, u32[]{:S(2)}) collective-permute-start(f32[138,5]{0,1:T(8,128)S(1)} %get-tuple-element.733), channel_id=1, source_target_pairs={{0,1},{1,2},{2,3},{4,5},{5,6},{6,7},{8,9},{9,10},{10,11},{12,13},{... | collective-permute-start | bytes 8288 | tf_op jit(solution)/shard_map/ppermute | solution.py:20
  30.2 8.0 %collective-permute-start.3 = (f32[138,5]{0,1:T(8,128)S(1)}, f32[138,5]{0,1:T(8,128)S(1)}, u32[]{:S(2)}, u32[]{:S(2)}) collective-permute-start(f32[138,5]{0,1:T(8,128)S(1)} %get-tuple-element.734), channel_id=1, source_target_pairs={{1,0},{2,1},{3,2},{5,4},{6,5},{7,6},{9,8},{10,9},{11,10},{13,12},{... | collective-permute-start | bytes 8288 | tf_op jit(solution)/shard_map/ppermute | solution.py:21
  32.3 6.1 %collective-permute-start.8 = (f32[136,4]{0,1:T(4,128)S(1)}, f32[136,4]{0,1:T(4,128)S(1)}, u32[]{:S(2)}, u32[]{:S(2)}) collective-permute-start(f32[136,4]{0,1:T(4,128)S(1)} %get-tuple-element.731), channel_id=1, source_target_pairs={{0,1},{1,2},{2,3},{4,5},{5,6},{6,7},{8,9},{9,10},{10,11},{12,13},{... | collective-permute-start | bytes 6536 | tf_op jit(solution)/shard_map/ppermute | solution.py:20
  36.1 5.5 %collective-permute-start.9 = (f32[136,4]{0,1:T(4,128)S(1)}, f32[136,4]{0,1:T(4,128)S(1)}, u32[]{:S(2)}, u32[]{:S(2)}) collective-permute-start(f32[136,4]{0,1:T(4,128)S(1)} %get-tuple-element.732), channel_id=1, source_target_pairs={{1,0},{2,1},{3,2},{5,4},{6,5},{7,6},{9,8},{10,9},{11,10},{13,12},{... | collective-permute-start | bytes 6536 | tf_op jit(solution)/shard_map/ppermute | solution.py:21
  45.8 15.1 %copy-start.2 = (f32[4096]{0:T(1024)S(1)}, f32[4096]{0:T(1024)}, u32[]{:S(2)}) copy-start(f32[4096]{0:T(1024)} %param.35) | copy-start | bytes 49156
  61.3 10.9 %collective-permute-start.10 = (f32[32,3,128]{2,0,1:T(8,128)S(1)}, f32[32,3,128]{2,0,1:T(8,128)S(1)}, u32[]{:S(2)}, u32[]{:S(2)}) collective-permute-start(f32[32,3,128]{2,0,1:T(8,128)S(1)} %get-tuple-element.752), channel_id=1, source_target_pairs={{4,0},{8,4},{12,8},{16,12},{20,16},{24,20},{28,24},{32,28},{36,32}... | collective-permute-start | bytes 147464 | tf_op jit(solution)/shard_map/ppermute | solution.py:29
  64.6 7.6 %collective-permute-start.11 = (f32[32,3,128]{2,0,1:T(8,128)S(1)}, f32[32,3,128]{2,0,1:T(8,128)S(1)}, u32[]{:S(2)}, u32[]{:S(2)}) collective-permute-start(f32[32,3,128]{2,0,1:T(8,128)S(1)} %get-tuple-element.751), channel_id=1, source_target_pairs={{0,4},{4,8},{8,12},{12,16},{16,20},{20,24},{24,28},{28,32},{32,36}... | collective-permute-start | bytes 147464 | tf_op jit(solution)/shard_map/ppermute | solution.py:29
  67.3 9.1 %all-to-all-start = ((s32[3,32,128]{2,0,1:T(4,128)}), s32[3,32,128]{2,0,1:T(4,128)S(1)}, u32[]{:S(2)}, u32[]{:S(2)}) async-start(s32[3,32,128]{2,0,1:T(4,128)} %copy.128), calls=%async_computation | async-start | bytes 131072 | tf_op jit(solution)/shard_map/all_to_all | solution.py:79
  76.4 9.7 %all-to-all-start.1 = ((f32[3,32,3,128]{3,2,0,1:T(4,128)}), f32[3,32,3,128]{3,2,0,1:T(4,128)S(1)}, u32[]{:S(2)}, u32[]{:S(2)}) async-start(f32[3,32,3,128]{3,2,0,1:T(4,128)} %copy.134), calls=%async_computation.1 | async-start | bytes 393216 | tf_op jit(solution)/shard_map/all_to_all | solution.py:89
  134.1 12.0 %collective-permute-start.12 = (f32[513]{0:T(1024)S(1)}, f32[513]{0:T(1024)S(1)}, u32[]{:S(2)}, u32[]{:S(2)}) collective-permute-start(f32[513]{0:T(1024)S(1)} %slice_reduce_fusion.1), channel_id=1, source_target_pairs={{0,4},{4,8},{8,12},{12,16},{16,20},{20,24},{24,28},{28,32},{32,36}... | collective-permute-start | bytes 6164 | tf_op jit(solution)/shard_map/ppermute | solution.py:29
  150.1 26.6 %collective-permute-start.13 = (f32[128]{0:T(128)S(1)}, f32[128]{0:T(128)S(1)}, u32[]{:S(2)}, u32[]{:S(2)}) collective-permute-start(f32[128]{0:T(128)S(1)} %slice_bitcast_fusion.4), channel_id=1, source_target_pairs={{0,1},{1,2},{2,3},{4,5},{5,6},{6,7},{8,9},{9,10},{10,11},{12,13},{... | collective-permute-start | bytes 1544 | tf_op jit(solution)/shard_map/ppermute | solution.py:29
  177.5 9.8 %collective-permute-start.14 = (f32[4,512]{0,1:T(8,128)S(1)}, f32[4,512]{0,1:T(8,128)S(1)}, u32[]{:S(2)}, u32[]{:S(2)}) collective-permute-start(f32[4,512]{0,1:T(8,128)S(1)} %get-tuple-element.735), channel_id=1, source_target_pairs={{0,4},{4,8},{8,12},{12,16},{16,20},{20,24},{24,28},{28,32},{32,36}... | collective-permute-start | bytes 24584 | tf_op jit(solution)/shard_map/ppermute | solution.py:20
  179.5 9.6 %collective-permute-start.15 = (f32[4,512]{0,1:T(8,128)S(1)}, f32[4,512]{0,1:T(8,128)S(1)}, u32[]{:S(2)}, u32[]{:S(2)}) collective-permute-start(f32[4,512]{0,1:T(8,128)S(1)} %get-tuple-element.736), channel_id=1, source_target_pairs={{4,0},{8,4},{12,8},{16,12},{20,16},{24,20},{28,24},{32,28},{36,32}... | collective-permute-start | bytes 24584 | tf_op jit(solution)/shard_map/ppermute | solution.py:21
  189.2 5.8 %collective-permute-start.16 = (f32[136,4]{0,1:T(4,128)S(1)}, f32[136,4]{0,1:T(4,128)S(1)}, u32[]{:S(2)}, u32[]{:S(2)}) collective-permute-start(f32[136,4]{0,1:T(4,128)S(1)} %get-tuple-element.729), channel_id=1, source_target_pairs={{0,1},{1,2},{2,3},{4,5},{5,6},{6,7},{8,9},{9,10},{10,11},{12,13},{... | collective-permute-start | bytes 6536 | tf_op jit(solution)/shard_map/ppermute | solution.py:20
  191.1 5.5 %collective-permute-start.17 = (f32[136,4]{0,1:T(4,128)S(1)}, f32[136,4]{0,1:T(4,128)S(1)}, u32[]{:S(2)}, u32[]{:S(2)}) collective-permute-start(f32[136,4]{0,1:T(4,128)S(1)} %get-tuple-element.730), channel_id=1, source_target_pairs={{1,0},{2,1},{3,2},{5,4},{6,5},{7,6},{9,8},{10,9},{11,10},{13,12},{... | collective-permute-start | bytes 6536 | tf_op jit(solution)/shard_map/ppermute | solution.py:21
  215.8 6.7 %collective-permute-start.18 = (f32[32,3,128]{2,0,1:T(8,128)S(1)}, f32[32,3,128]{2,0,1:T(8,128)S(1)}, u32[]{:S(2)}, u32[]{:S(2)}) collective-permute-start(f32[32,3,128]{2,0,1:T(8,128)S(1)} %get-tuple-element.746), channel_id=1, source_target_pairs={{4,0},{8,4},{12,8},{16,12},{20,16},{24,20},{28,24},{32,28},{36,32}... | collective-permute-start | bytes 147464 | tf_op jit(solution)/shard_map/ppermute | solution.py:29
  220.5 7.5 %collective-permute-start.19 = (f32[32,3,128]{2,0,1:T(8,128)S(1)}, f32[32,3,128]{2,0,1:T(8,128)S(1)}, u32[]{:S(2)}, u32[]{:S(2)}) collective-permute-start(f32[32,3,128]{2,0,1:T(8,128)S(1)} %get-tuple-element.745), channel_id=1, source_target_pairs={{0,4},{4,8},{8,12},{12,16},{16,20},{20,24},{24,28},{28,32},{32,36}... | collective-permute-start | bytes 147464 | tf_op jit(solution)/shard_map/ppermute | solution.py:29
  228.9 9.9 %all-to-all-start.2 = ((f32[3,32,3,128]{3,2,0,1:T(4,128)}), f32[3,32,3,128]{3,2,0,1:T(4,128)S(1)}, u32[]{:S(2)}, u32[]{:S(2)}) async-start(f32[3,32,3,128]{3,2,0,1:T(4,128)} %copy.141), calls=%async_computation.2 | async-start | bytes 393216 | tf_op jit(solution)/shard_map/all_to_all | solution.py:89
  286.9 7.0 %collective-permute-start.20 = (f32[513]{0:T(1024)S(1)}, f32[513]{0:T(1024)S(1)}, u32[]{:S(2)}, u32[]{:S(2)}) collective-permute-start(f32[513]{0:T(1024)S(1)} %slice_reduce_fusion), channel_id=1, source_target_pairs={{0,4},{4,8},{8,12},{12,16},{16,20},{20,24},{24,28},{28,32},{32,36}... | collective-permute-start | bytes 6164 | tf_op jit(solution)/shard_map/ppermute | solution.py:29
  297.8 5.5 %collective-permute-start.21 = (f32[128]{0:T(128)S(1)}, f32[128]{0:T(128)S(1)}, u32[]{:S(2)}, u32[]{:S(2)}) collective-permute-start(f32[128]{0:T(128)S(1)} %slice_bitcast_fusion.3), channel_id=1, source_target_pairs={{0,1},{1,2},{2,3},{4,5},{5,6},{6,7},{8,9},{9,10},{10,11},{12,13},{... | collective-permute-start | bytes 1544 | tf_op jit(solution)/shard_map/ppermute | solution.py:29
where the time goes:
time: 306 us; the launch traced here: 305 us
  matrix products  107 us (35%)
  starting transfers between devices  79.3 us (26%)
  waiting for transfers between devices  34.9 us (11%)
  blocking collectives  32.7 us (11%)
  other arithmetic  27 us (9%)
  local copies, waits for them, and re-layouts  17.5 us (6%)
  loops' own time  4.48 us (1%)
    dot_general x48, matrix products, step(): lax.dot_general(row_side, col_side, (((0,), (0,)), ((), ())), precision=l...  89 us
    psum x4, blocking collectives, one_axis_at_a_time(): value = lax.psum(value, axis)  32.7 us
    ppermute x6, starting transfers between devices, padded_2(): after = lax.ppermute(initial, axis, down)  25.2 us
    ppermute x10, starting transfers between devices, from_behind(): lax.ppermute(value, axis, [(source, source + steps) for source in range(i...  23.9 us
    dot_general x16, matrix products, step(): jnp.dot(picks, padded, precision=lax.Precision.HIGHEST, preferred_element...  17.1 us
    ppermute x6, starting transfers between devices, padded_2(): before = lax.ppermute(last, axis, up)  15.3 us
    ppermute x10, waiting for transfers between devices, from_behind(): lax.ppermute(value, axis, [(source, source + steps) for source in range(i...  13.2 us
    all_to_all x2, starting transfers between devices, route_moves(): lax.all_to_all(gathered, 'cols', split_axis=1, concat_axis=1, tiled=True)  9.86 us
  transfers between devices with their start and end apart: 25, of which 10 were waited for; matrix products, arithmetic and copies ran while one was open for 9% of the time, Pallas kernels for 0%

commit v1 on v0

v1 whole, which is shorter than its diff:
```python
import functools

import jax
import jax.numpy as jnp
from jax import lax
from jax.experimental import pallas as pl
from jax.experimental.pallas import tpu as pltpu
from jax.sharding import PartitionSpec as P

HJB_STEPS = 4
ITERS = 2
CAP = 8
RT = 16
LT = 4
DR = 144
F32 = jnp.float32
BF16 = jnp.bfloat16
I16 = jnp.int16
GROUP = 12
SELF = 4


def hjb_step(src, dst, den, lane, sub, row_in, side_in):
    tiles, n_t, n_j = {}, RT + 2, LT + 1
    rolled = {}

    def cell(t, j):
        if (t, j) not in tiles:
            tiles[t, j] = src[t, :, 128 * j : 128 * j + 128]
        return tiles[t, j]

    def roll(t, j, shift, axis):
        key = (t, j, shift, axis)
        if key not in rolled:
            rolled[key] = pltpu.roll(cell(t, j), shift, axis)
        return rolled[key]

    for t in range(n_t):
        for j in range(n_j):
            v = cell(t, j)
            up = jnp.where(sub == 0, roll((t - 1) % n_t, j, 1, 0), roll(t, j, 1, 0))
            down = jnp.where(sub == 7, roll((t + 1) % n_t, j, 7, 0), roll(t, j, 7, 0))
            left = jnp.where(lane == 0, roll(t, (j - 1) % n_j, 1, 1), roll(t, j, 1, 1))
            right = jnp.where(lane == 127, roll(t, (j + 1) % n_j, 127, 1), roll(t, j, 127, 1))
            px = jnp.maximum(v - jnp.minimum(up, down), 0.0)
            py = jnp.maximum(v - jnp.minimum(left, right), 0.0)
            spread = up + down + left + right - 4.0 * v
            d = den[t, :, 128 * j : 128 * j + 128]
            new = v + 0.25 * (0.5 * spread - 0.5 * (px * px + py * py) + 0.5 * d)
            if t >= RT:
                new = jnp.where(row_in[t - RT], new, 0.0)
            if j == LT:
                new = jnp.where(side_in, new, 0.0)
            dst[t, :, 128 * j : 128 * j + 128] = new


def sample(u, u1, cells, corners):
    zero = jnp.zeros((8, 128), F32)

    def agents(a, carry):
        cell = cells[a]
        key = cell >> 7
        idx = cell & 127
        u00, u10, u01, u11 = zero, zero, zero, zero
        for r in range(8 * RT + 1):
            for j in range(LT):
                part = (r // 8, slice(r % 8, r % 8 + 1), slice(128 * j, 128 * j + 128))
                here = jnp.take_along_axis(jnp.broadcast_to(u[part], (8, 128)), idx, axis=1)
                next_ = jnp.take_along_axis(jnp.broadcast_to(u1[part], (8, 128)), idx, axis=1)
                if r < 8 * RT:
                    hit = key == r * LT + j
                    u00 = jnp.where(hit, here, u00)
                    u01 = jnp.where(hit, next_, u01)
                if r > 0:
                    hit = key == (r - 1) * LT + j
                    u10 = jnp.where(hit, here, u10)
                    u11 = jnp.where(hit, next_, u11)
        for n, v in enumerate((u00, u10, u01, u11)):
            corners[n, a] = v
        return carry

    lax.fori_loop(0, 4, agents, 0)


def exact_parts(v):
    high = v.astype(BF16)
    rest = v - high.astype(F32)
    mid = rest.astype(BF16)
    return high, mid, (rest - mid.astype(F32)).astype(BF16)


def place(placing, v):
    out = None
    for part in exact_parts(v):
        term = jnp.dot(placing, part, preferred_element_type=F32)
        out = term if out is None else out + term
    return out


def build_and_add(static, moves, lhs, hot, acc):
    cell = static[0].astype(jnp.int32)
    mass = static[1]
    x, y = moves[0], moves[1]
    row, col = cell >> 9, cell & 511
    upper, lower = mass * (1.0 - x), mass * x
    row_iota = lax.broadcasted_iota(I16, (DR, 128), 0)
    col_iota = lax.broadcasted_iota(I16, (512, 128), 0)
    parts = []
    for v in (upper * (1.0 - y), lower * (1.0 - y), upper * y, lower * y):
        high = v.astype(BF16).astype(F32)
        parts.append((high, v - high))

    def spread(v, b, dtype, copies):
        tile = jnp.broadcast_to(v[b : b + 1], (16, 128)).astype(dtype)
        return jnp.tile(tile, (copies, 1))

    for b in range(CAP):
        r = spread(row, b, I16, DR // 16)
        q = spread(col, b, I16, 32)
        on_upper = row_iota == r
        on_lower = row_iota == r + I16(1)
        for kind in range(2):
            for p in range(2):
                v = spread(parts[2 * kind][p], b, BF16, DR // 16)
                w = spread(parts[2 * kind + 1][p], b, BF16, DR // 16)
                lhs[pl.ds((2 * kind + p) * DR, DR), pl.ds(128 * b, 128)] = jnp.where(
                    on_upper, v, jnp.where(on_lower, w, BF16(0))
                )
        hot[:, pl.ds(128 * b, 128)] = jnp.where(col_iota == q, BF16(1), BF16(0))
    acc[...] += lax.dot_general(
        lhs[...], hot[...], (((1,), (1,)), ((), ())), preferred_element_type=F32
    )


def kernel(
    n_rows, n_cols,
    u_in, m_in, cells_in, off_in, w_in, dest_in, end_in,
    value_out, density_out,
    um, ua, ub, grid, cells, off_raw, off, frac, w, ends, dest, corners,
    side_send, side_recv, corner_recv,
    static_send, static_recv, move_send, move_recv,
    lhs, hot, acc,
    g_side_l, g_side_r, g_from_u, g_from_d, g_from_l, g_from_r, g_from_ul, g_from_ur, g_from_dl, g_from_dr,
    red_send, red_recv, result,
    load_sem, out_sem,
    halo_s, halo_r, static_s, static_r, move_s, move_r, g_s, g_r, red_s, red_r,
):
    row = lax.axis_index("rows")
    col = lax.axis_index("cols")

    def at(dr, dc):
        return (lax.rem(row + dr + n_rows, n_rows), lax.rem(col + dc + n_cols, n_cols))

    def remote(src, dst, s, r, to):
        return pltpu.make_async_remote_copy(
            src_ref=src, dst_ref=dst, send_sem=s, recv_sem=r,
            device_id=to, device_id_type=pl.DeviceIdType.MESH,
        )

    loads = [
        (u_in, um.at[0, pl.ds(0, RT), :, pl.ds(0, 512)]),
        (m_in, um.at[1, pl.ds(0, RT), :, pl.ds(0, 512)]),
        (dest_in, dest), (w_in, w), (end_in, ends), (off_in, off_raw), (cells_in, cells),
    ]
    loads = [pltpu.make_async_copy(a, b, load_sem.at[i]) for i, (a, b) in enumerate(loads)]
    for c in loads:
        c.start()

    group = [(dr, k) for dr in (-1, 0, 1) for k in range(n_cols)]
    near = row % 8
    base = row - near
    row_peers = [base + (near + j) % 8 for j in range(1, 8)]
    far_peers = [lax.rem(row + 8 * j, n_rows) for j in range(1, 4)]

    barrier = pltpu.get_barrier_semaphore()
    greet = [at(dr, k) for dr, k in group if (dr, k) != (0, 0)]
    greet += [(p, col) for p in row_peers + far_peers]
    for to in greet:
        pl.semaphore_signal(barrier, inc=1, device_id=to, device_id_type=pl.DeviceIdType.MESH)

    lane = lax.broadcasted_iota(jnp.int32, (8, 128), 1)
    sub = lax.broadcasted_iota(jnp.int32, (8, 128), 0)
    has_up, has_down = row > 0, row < n_rows - 1
    has_left, has_right = col > 0, col < n_cols - 1
    row_in = (has_down, has_up)
    lane_right = lane < jnp.where(has_right, 8, 0)
    lane_left = lane >= jnp.where(has_left, 120, 128)
    side_in = lane_right | lane_left

    for c in loads[:2]:
        c.wait()
    for v in range(2):
        first = um[v, 0:RT, :, 0:128].reshape(128, 128).T
        last = um[v, 0:RT, :, 384:512].reshape(128, 128).T
        side_send[0, v] = first[0:8]
        side_send[1, v] = last[120:128]
    pl.semaphore_wait(barrier, len(greet))

    halo = [
        remote(um.at[:, 0, :, pl.ds(0, 512)], um.at[:, RT, :, pl.ds(0, 512)], halo_s.at[0], halo_r.at[0], at(-1, 0)),
        remote(um.at[:, RT - 1, :, pl.ds(0, 512)], um.at[:, RT + 1, :, pl.ds(0, 512)], halo_s.at[1], halo_r.at[1], at(1, 0)),
        remote(um.at[:, 0, :, pl.ds(0, 128)], corner_recv.at[0], halo_s.at[2], halo_r.at[2], at(-1, -1)),
        remote(um.at[:, 0, :, pl.ds(384, 128)], corner_recv.at[1], halo_s.at[3], halo_r.at[3], at(-1, 1)),
        remote(um.at[:, RT - 1, :, pl.ds(0, 128)], corner_recv.at[2], halo_s.at[4], halo_r.at[4], at(1, -1)),
        remote(um.at[:, RT - 1, :, pl.ds(384, 128)], corner_recv.at[3], halo_s.at[5], halo_r.at[5], at(1, 1)),
        remote(side_send.at[0], side_recv.at[0], halo_s.at[6], halo_r.at[6], at(0, -1)),
        remote(side_send.at[1], side_recv.at[1], halo_s.at[7], halo_r.at[7], at(0, 1)),
    ]
    for c in halo:
        c.start()

    loads[3].wait()
    red_send[0] = w[0] + w[1] + w[2] + w[3]
    stages = [
        [(0, at(0, k)) for k in range(1, n_cols)],
        [(1, (p, col)) for p in row_peers],
        [(2, (p, col)) for p in far_peers],
    ]
    red, count = [], 0
    for stage in stages:
        copies = []
        for s, to in stage:
            copies.append(remote(red_send.at[s], red_recv.at[count], red_s.at[count], red_r.at[count], to))
            count += 1
        red.append(copies)
    for c in red[0]:
        c.start()

    def reduce_stage(s):
        total, first = red_send[s], sum(len(x) for x in red[:s])
        for i, c in enumerate(red[s]):
            c.wait()
            total = total + red_recv[first + i]
        if s + 1 < len(red):
            red_send[s + 1] = total
            for c in red[s + 1]:
                c.start()
        return total

    loads[2].wait()
    d = dest[...]
    along = jnp.broadcast_to(d.astype(F32), (32, 32))
    same = along == along.T
    order_b = lax.broadcasted_iota(jnp.int32, (32, 32), 0)
    order_a = lax.broadcasted_iota(jnp.int32, (32, 32), 1)
    rank = jnp.sum(jnp.where(same & (order_b < order_a), 1.0, 0.0), axis=0, keepdims=True).astype(jnp.int32)
    slot = ((d >> 2) - row + 1) * (n_cols * CAP) + (((d & 3) - col) & 3) * CAP + rank
    slot_iota = lax.broadcasted_iota(jnp.int32, (GROUP * CAP, 32), 0)
    placing = jnp.where(slot_iota == slot, 1.0, 0.0).astype(BF16)

    def send_group(send, recv, ss, rs):
        copies = {}
        for i, (dr, k) in enumerate(group):
            if i != SELF:
                copies[i] = remote(send.at[i], recv.at[i], ss.at[i], rs.at[i], at(dr, k))
                copies[i].start()
        return copies

    loads[4].wait()
    block_static = jnp.concatenate(
        [ends[...].reshape(32, 128).astype(F32), w[...].reshape(32, 128)], axis=1
    )
    placed = place(placing, block_static)
    for n in range(2):
        static_send[:, n] = placed[:, 128 * n : 128 * n + 128].reshape(GROUP, CAP, 128)
    for n in range(2):
        static_recv[SELF, n] = placed[SELF * CAP : SELF * CAP + CAP, 128 * n : 128 * n + 128]
    static_copies = send_group(static_send, static_recv, static_s, static_r)

    loads[5].wait()
    loads[6].wait()
    for b in range(32):
        both = off_raw[:, 128 * b : 128 * b + 128]
        for n in range(2):
            off[n, b // 8, b % 8 : b % 8 + 1, :] = both[n : n + 1]
    for n in range(2):
        frac[n] = 0.5 + 0.45 * jnp.tanh(off[n])

    for c in halo:
        c.wait()
    zero_mid = jnp.zeros((112, 128), F32)
    for v in range(2):
        strip = jnp.concatenate([side_recv[0, v], zero_mid, side_recv[1, v]], axis=0).T
        strip = strip.reshape(RT, 8, 128)
        um[v, 0:RT, :, 512:640] = jnp.where(side_in, strip, 0.0) if v == 0 else strip
        below = jnp.where(lane < 64, corner_recv[0, v], corner_recv[1, v])
        above = jnp.where(lane < 64, corner_recv[2, v], corner_recv[3, v])
        if v == 0:
            below = jnp.where(side_in & has_down, below, 0.0)
            above = jnp.where(side_in & has_up, above, 0.0)
            um[0, RT, :, 0:512] = jnp.where(has_down, um[0, RT, :, 0:512], 0.0)
            um[0, RT + 1, :, 0:512] = jnp.where(has_up, um[0, RT + 1, :, 0:512], 0.0)
        um[v, RT, :, 512:640] = below
        um[v, RT + 1, :, 512:640] = above

    def exchange(it):
        full = it + 1 < ITERS
        ss, rs = g_s.at[it], g_r.at[it]
        third = grid[0:RT, :, 384:512].reshape(128, 128).T
        fourth = grid[0:RT, :, 512:640].reshape(128, 128).T
        g_side_r[it, 0] = third[120:128]
        g_side_r[it, 1] = fourth[0:8]
        g_side_r[it, 2] = grid[RT, :, 384:512]
        g_side_r[it, 3] = grid[RT, :, 512:640]
        if full:
            first = grid[0:RT, :, 0:128].reshape(128, 128).T
            g_side_l[0] = first[0:8]
            g_side_l[1] = grid[RT, :, 0:128]
        copies = [
            remote(grid.at[pl.ds(RT - 1, 2)], g_from_u.at[it], ss.at[0], rs.at[0], at(1, 0)),
            remote(g_side_r.at[it], g_from_l.at[it], ss.at[1], rs.at[1], at(0, 1)),
            remote(grid.at[pl.ds(RT - 1, 2), :, pl.ds(384, 256)], g_from_ul.at[it], ss.at[2], rs.at[2], at(1, 1)),
        ]
        if full:
            copies += [
                remote(grid.at[0], g_from_d, ss.at[3], rs.at[3], at(-1, 0)),
                remote(g_side_l, g_from_r, ss.at[4], rs.at[4], at(0, -1)),
                remote(grid.at[pl.ds(RT - 1, 2), :, pl.ds(0, 128)], g_from_ur, ss.at[5], rs.at[5], at(1, -1)),
                remote(grid.at[0, :, pl.ds(384, 256)], g_from_dl, ss.at[6], rs.at[6], at(-1, 1)),
                remote(grid.at[0, :, pl.ds(0, 128)], g_from_dr, ss.at[7], rs.at[7], at(-1, -1)),
            ]
        for c in copies:
            c.start()
        return copies

    def gather_edges(it):
        full = it + 1 < ITERS
        top = sub == 0
        left0 = (lane == 0) & has_left
        l4, z = slice(512, 640), 0.0
        grid[RT + 1] = jnp.where(has_up, g_from_u[it, 0], z)
        for j in range(LT + 1):
            js = slice(128 * j, 128 * j + 128)
            grid[0, :, js] += jnp.where(top & has_up, g_from_u[it, 1, :, js], z)
        if full:
            grid[RT] += jnp.where(has_down, g_from_d[...], z)
        right_rows = g_from_r[0] if full else jnp.zeros((8, 128), F32)
        strip = jnp.concatenate([right_rows, zero_mid, g_from_l[it, 0]], axis=0).T.reshape(RT, 8, 128)
        grid[0:RT, :, l4] += jnp.where(side_in, strip, z)
        spill = jnp.concatenate([g_from_l[it, 1], jnp.zeros((120, 128), F32)], axis=0).T.reshape(RT, 8, 128)
        grid[0:RT, :, 0:128] += jnp.where(left0, spill, z)
        edge = jnp.where(lane_left, g_from_l[it, 2], z)
        if full:
            edge = edge + jnp.where(lane_right, g_from_r[1], z)
        grid[RT, :, l4] += edge
        grid[RT, :, 0:128] += jnp.where(left0, g_from_l[it, 3], z)
        corner = jnp.where(lane_left, g_from_ul[it, 0, :, 0:128], z)
        corner_top = jnp.where(lane_left, g_from_ul[it, 1, :, 0:128], z)
        if full:
            corner = corner + jnp.where(lane_right, g_from_ur[0], z)
            corner_top = corner_top + jnp.where(lane_right, g_from_ur[1], z)
        grid[RT + 1, :, l4] += jnp.where(has_up, corner, z)
        grid[RT + 1, :, 0:128] += jnp.where(left0 & has_up, g_from_ul[it, 0, :, 128:256], z)
        grid[0, :, l4] += jnp.where(top & has_up, corner_top, z)
        grid[0, :, 0:128] += jnp.where(top & left0 & has_up, g_from_ul[it, 1, :, 128:256], z)
        if full:
            corner = jnp.where(lane_left, g_from_dl[:, 0:128], z) + jnp.where(lane_right, g_from_dr[...], z)
            grid[RT, :, l4] += jnp.where(has_down, corner, z)
            grid[RT, :, 0:128] += jnp.where(left0 & has_down, g_from_dl[:, 128:256], z)
        for j in range(LT + 1):
            js = slice(128 * j, 128 * j + 128)
            folded = pltpu.roll(grid[RT, :, js], 7, 0)
            grid[RT - 1, :, js] += jnp.where((sub == 7) & jnp.logical_not(has_down), folded, z)
        for t in range(RT + 2):
            folded = pltpu.roll(grid[t, :, l4], 127, 1)
            grid[t, :, 384:512] += jnp.where((lane == 127) & jnp.logical_not(has_right), folded, z)

    scale = None
    for it in range(ITERS):
        hjb = functools.partial(hjb_step, lane=lane, sub=sub, row_in=row_in, side_in=side_in)
        den = um.at[1]
        hjb(um.at[0], ua, den)
        hjb(ua, ub, den)
        hjb(ub, ua, den)
        hjb(ua, ub, den)
        if it == 0:
            reduce_stage(0)
        else:
            value_copy = pltpu.make_async_copy(ub.at[pl.ds(0, RT), :, pl.ds(0, 512)], value_out, out_sem.at[0])
            value_copy.start()
        ua[0 : RT + 1] = pltpu.roll(ub[0 : RT + 1].reshape(8 * RT + 8, 640), 639, 1).reshape(RT + 1, 8, 640)
        sample(ub, ua, cells, corners)
        dx0, dx1 = corners[1] - corners[0], corners[3] - corners[2]
        dy0, dy1 = corners[2] - corners[0], corners[3] - corners[1]
        fx, fy = frac[0], frac[1]
        gx = (1.0 - fy) * dx0 + fy * dx1
        gy = (1.0 - fx) * dy0 + fx * dy1
        hx = 0.5 + 0.45 * jnp.tanh(off[0] - gx)
        hy = 0.5 + 0.45 * jnp.tanh(off[1] - gy)
        placed = place(placing, jnp.concatenate([hx.reshape(32, 128), hy.reshape(32, 128)], axis=1))
        for n in range(2):
            move_send[it, :, n] = placed[:, 128 * n : 128 * n + 128].reshape(GROUP, CAP, 128)
            move_recv[it, SELF, n] = placed[SELF * CAP : SELF * CAP + CAP, 128 * n : 128 * n + 128]
        move_copies = send_group(move_send.at[it], move_recv.at[it], move_s.at[it], move_r.at[it])
        acc[...] = jnp.zeros_like(acc)
        if it == 0:
            reduce_stage(1)

        def arrivals(i, carry):
            s = lax.rem(i + SELF, GROUP)

            @pl.when(i > 0)
            def _():
                remote(move_send.at[it, s], move_recv.at[it, s], move_s.at[it, s], move_r.at[it, s], at(0, 1)).wait_recv()
                if it == 0:
                    remote(static_send.at[s], static_recv.at[s], static_s.at[s], static_r.at[s], at(0, 1)).wait_recv()

            build_and_add(static_recv[s], move_recv[it, s], lhs, hot, acc)
            return carry

        lax.fori_loop(0, GROUP, arrivals, 0)
        zero = jnp.zeros((DR, 128), F32)
        here = acc[0:DR] + acc[DR : 2 * DR]
        beside = acc[2 * DR : 3 * DR] + acc[3 * DR : 4 * DR]
        whole = jnp.concatenate([here, zero], axis=1) + pltpu.roll(jnp.concatenate([beside, zero], axis=1), 1, 1)
        grid[...] = whole.reshape(RT + 2, 8, 640)
        copies = exchange(it)
        if it == 0:
            total = reduce_stage(2)
            scale = jnp.float32(n_rows * n_cols * 128 * 512) / jnp.sum(total, keepdims=True)
        for c in list(move_copies.values()) + (list(static_copies.values()) if it == 0 else []):
            c.wait_send()
        for c in copies:
            c.wait()
        gather_edges(it)
        if it + 1 < ITERS:
            um[1] = 0.5 * um[1] + 0.5 * (grid[...] * scale.reshape(1, 1, 1))
        else:
            result[...] = 0.5 * um[1, 0:RT, :, 0:512] + 0.5 * (grid[0:RT, :, 0:512] * scale.reshape(1, 1, 1))
            density_copy = pltpu.make_async_copy(result, density_out, out_sem.at[1])
            density_copy.start()
            value_copy.wait()
            density_copy.wait()


def body(n_rows, n_cols, terminal_value, density_start, start_cells, offsets, weights, dest_tiles, end_cells):
    any_ = pl.BlockSpec(memory_space=pl.ANY)
    vmem = pltpu.VMEM
    dma = pltpu.SemaphoreType.DMA
    tile = jax.ShapeDtypeStruct((RT, 8, 512), F32)
    value, density = pl.pallas_call(
        functools.partial(kernel, n_rows, n_cols),
        out_shape=(tile, tile),
        in_specs=[any_] * 7,
        out_specs=(any_, any_),
        scratch_shapes=[
            vmem((2, RT + 2, 8, 640), F32), vmem((RT + 2, 8, 640), F32), vmem((RT + 2, 8, 640), F32),
            vmem((RT + 2, 8, 640), F32),
            vmem((4, 8, 128), jnp.int32), vmem((2, 4096), F32), vmem((2, 4, 8, 128), F32), vmem((2, 4, 8, 128), F32),
            vmem((4, 8, 128), F32), vmem((4, 8, 128), jnp.int32), vmem((1, 32), jnp.int32), vmem((4, 4, 8, 128), F32),
            vmem((2, 2, 8, 128), F32), vmem((2, 2, 8, 128), F32), vmem((4, 2, 8, 128), F32),
            vmem((GROUP, 2, CAP, 128), F32), vmem((GROUP, 2, CAP, 128), F32),
            vmem((ITERS, GROUP, 2, CAP, 128), F32), vmem((ITERS, GROUP, 2, CAP, 128), F32),
            vmem((4 * DR, 1024), BF16), vmem((512, 1024), BF16), vmem((4 * DR, 512), F32),
            vmem((2, 8, 128), F32), vmem((ITERS, 4, 8, 128), F32),
            vmem((ITERS, 2, 8, 640), F32), vmem((8, 640), F32), vmem((ITERS, 4, 8, 128), F32), vmem((2, 8, 128), F32),
            vmem((ITERS, 2, 8, 256), F32), vmem((2, 8, 128), F32), vmem((8, 256), F32), vmem((8, 128), F32),
            vmem((3, 8, 128), F32), vmem((13, 8, 128), F32), vmem((RT, 8, 512), F32),
            dma((7,)), dma((2,)),
            dma((8,)), dma((8,)), dma((GROUP,)), dma((GROUP,)),
            dma((ITERS, GROUP)), dma((ITERS, GROUP)), dma((ITERS, 8)), dma((ITERS, 8)), dma((13,)), dma((13,)),
        ],
        compiler_params=pltpu.CompilerParams(collective_id=0, has_side_effects=True),
        name="crowd",
    )(
        terminal_value.reshape(RT, 8, 512),
        density_start.reshape(RT, 8, 512),
        start_cells.reshape(4, 8, 128),
        offsets,
        weights.reshape(4, 8, 128),
        dest_tiles.reshape(1, 32),
        end_cells.reshape(4, 8, 128),
    )
    return value.reshape(128, 512), density.reshape(128, 512)


def solution(mesh):
    both = ("rows", "cols")
    return jax.shard_map(
        functools.partial(body, mesh.shape["rows"], mesh.shape["cols"]),
        mesh=mesh,
        in_specs=(P("rows", "cols"), P("rows", "cols"), P(both), P(None, both), P(both), P(both), P(both)),
        out_specs=(P("rows", "cols"), P("rows", "cols")),
        check_vma=False,
    )
```

time: 306 us -> 68.2 us (0.22)
  the two profiles are of different devices: /device:TPU:40 before, /device:TPU:1 now
where the time goes in v1:
time: 68.2 us; the launch traced here: 68 us
  Pallas kernels  64.9 us (95%)
  local copies, waits for them, and re-layouts  2.42 us (4%)
    pallas_call x1, Pallas kernels, body(): pl.pallas_call(functools.partial(kernel, n_rows, n_cols), out_shape=(tile...  64.9 us
    unnamed x4, local copies, waits for them, and re-layouts  2.42 us

profile of v1, /device:TPU:1, one launch (start us, length us, event | category | flops | bytes accessed | tf_op | source)
XLA Modules:
  0.0 68.0 jit_solution(10120600110024110216)
XLA Ops:
  0.6 64.9 %crowd.1 = (f32[16,8,512]{2,1,0:T(8,128)}, f32[16,8,512]{2,1,0:T(8,128)}) custom-call(f32[16,8,512]{2,1,0:T(8,128)} %bitcast.8, f32[16,8,512]{2,1,0:T(8,128)} %bitcast.9, s32[4,8,128]{2,1,0:T(8,128)} %bitcast.12, f32[2,4096]{1,0:T(2,128)} %off_in.1, f32[4,8,128]{2,1,0:T(8,128)} %bitcast.13, s32[1,32]{1,0:T(1,128)} %bitcast.15, s32[4,8,128]{2,1,0:T(8,128)} %bitcast.14), custom_call_target="tpu_custom_call" | custom-call | tf_op jit(solution)/shard_map/crowd/pallas_call | solution.py:441
  65.6 0.0 copy-start
  65.6 1.7 %copy.11 = f32[128,512]{1,0:T(8,128)} copy(f32[128,512]{1,0:T(8,128)} %bitcast.11) | data formatting | bytes 524288
  67.3 0.0 copy-done
  67.3 0.7 %copy.12 = f32[128,512]{1,0:T(8,128)} copy(f32[128,512]{1,0:T(8,128)S(1)} %bitcast.10) | data formatting | bytes 524288
Async XLA Ops:
  65.6 1.7 %copy-start = (f32[16,8,512]{2,1,0:T(8,128)S(1)}, f32[16,8,512]{2,1,0:T(8,128)}, u32[]{:S(2)}) copy-start(f32[16,8,512]{2,1,0:T(8,128)} %get-tuple-element.5) | copy-start | bytes 786436

commit v2 on v1

--- a/solution.py
+++ b/solution.py
@@ -12,7 +12,7 @@
 CAP = 8
 RT = 16
 LT = 4
-DR = 144
+ORDER = ((1, 0), (2, 0), (1, 1), (1, 3), (2, 1), (2, 3), (0, 0), (1, 2), (2, 2), (0, 1), (0, 3), (0, 2))
 F32 = jnp.float32
 BF16 = jnp.bfloat16
 I16 = jnp.int16
@@ -54,31 +54,54 @@
             dst[t, :, 128 * j : 128 * j + 128] = new
 
 
-def sample(u, u1, cells, corners):
-    zero = jnp.zeros((8, 128), F32)
-
+def slopes(u, table, lane, sub):
+    def split(block, first, count):
+        turned = block.T[0:count]
+        high = turned.astype(BF16)
+        table[pl.ds(first, count), pl.ds(0, 128)] = high
+        table[pl.ds(first, count), pl.ds(128, 128)] = (turned - high.astype(F32)).astype(BF16)
+    for j in range(LT + 1):
+        js = slice(128 * j, 128 * j + 128)
+        tiles = [u[t, :, js] for t in range(RT + 1)]
+        ups = [pltpu.roll(x, 7, 0) for x in tiles]
+        dx = [jnp.where(sub == 7, ups[t + 1], ups[t]) - tiles[t] for t in range(RT)]
+        split(jnp.concatenate(dx, axis=0), 128 * j, 128 if j < LT else 16)
+        if j < LT:
+            dy = []
+            for t in range(RT):
+                near = pltpu.roll(tiles[t], 127, 1)
+                far = pltpu.roll(u[t, :, 128 * j + 128 : 128 * j + 256], 127, 1)
+                dy.append(jnp.where(lane == 127, far, near) - tiles[t])
+            split(jnp.concatenate(dy, axis=0), 528 + 128 * j, 128)
+
+
+def sample(table, cells, corners):
     def agents(a, carry):
         cell = cells[a]
-        key = cell >> 7
-        idx = cell & 127
-        u00, u10, u01, u11 = zero, zero, zero, zero
-        for r in range(8 * RT + 1):
-            for j in range(LT):
-                part = (r // 8, slice(r % 8, r % 8 + 1), slice(128 * j, 128 * j + 128))
-                here = jnp.take_along_axis(jnp.broadcast_to(u[part], (8, 128)), idx, axis=1)
-                next_ = jnp.take_along_axis(jnp.broadcast_to(u1[part], (8, 128)), idx, axis=1)
-                if r < 8 * RT:
-                    hit = key == r * LT + j
-                    u00 = jnp.where(hit, here, u00)
-                    u01 = jnp.where(hit, next_, u01)
-                if r > 0:
-                    hit = key == (r - 1) * LT + j
-                    u10 = jnp.where(hit, here, u10)
-                    u11 = jnp.where(hit, next_, u11)
-        for n, v in enumerate((u00, u10, u01, u11)):
-            corners[n, a] = v
+        row, col = cell >> 9, cell & 511
+        for h in range(2):
+            hot, places = [], []
+            for b in range(4 * h, 4 * h + 4):
+                r = jnp.tile(jnp.broadcast_to(row[b : b + 1], (16, 128)).astype(I16), (8, 1))
+                one = jnp.where(lax.broadcasted_iota(I16, (128, 128), 0) == r, BF16(1), BF16(0))
+                hot.append(jnp.concatenate([one, one], axis=0))
+                places.append(jnp.broadcast_to(col[b : b + 1], (8, 128)))
+            picked = jnp.dot(table[...], jnp.concatenate(hot, axis=1), preferred_element_type=F32)
+            place = jnp.concatenate(places, axis=1) - lax.broadcasted_iota(jnp.int32, (8, 512), 0)
+            zero = jnp.zeros((8, 512), F32)
+            d0, d1, e0 = zero, zero, zero
+            for i in range(64):
+                here = place == 8 * i
+                x = picked[8 * i : 8 * i + 8]
+                d0 = jnp.where(here, x, d0)
+                d1 = jnp.where(place == 8 * i - 1, x, d1)
+                e0 = jnp.where(here, picked[528 + 8 * i : 536 + 8 * i], e0)
+            d1 = jnp.where(place == 511, picked[512:520], d1)
+            for n, v in enumerate((d0, d1, e0)):
+                v = jnp.sum(v, axis=0, keepdims=True)
+                for b in range(4):
+                    corners[n, a, 4 * h + b : 4 * h + b + 1, :] = v[:, 128 * b : 128 * b + 128]
         return carry
-
     lax.fori_loop(0, 4, agents, 0)
 
 
@@ -97,14 +120,15 @@
     return out
 
 
-def build_and_add(static, moves, lhs, hot, acc):
+def deposit(static, moves, acc):
     cell = static[0].astype(jnp.int32)
     mass = static[1]
     x, y = moves[0], moves[1]
     row, col = cell >> 9, cell & 511
     upper, lower = mass * (1.0 - x), mass * x
-    row_iota = lax.broadcasted_iota(I16, (DR, 128), 0)
+    row_iota = lax.broadcasted_iota(I16, (128, 128), 0)
     col_iota = lax.broadcasted_iota(I16, (512, 128), 0)
+    spill_iota = lax.broadcasted_iota(I16, (16, 128), 0)
     parts = []
     for v in (upper * (1.0 - y), lower * (1.0 - y), upper * y, lower * y):
         high = v.astype(BF16).astype(F32)
@@ -112,23 +136,31 @@
 
     def spread(v, b, dtype, copies):
         tile = jnp.broadcast_to(v[b : b + 1], (16, 128)).astype(dtype)
-        return jnp.tile(tile, (copies, 1))
-
+        return jnp.tile(tile, (copies, 1)) if copies > 1 else tile
+
+    zero = BF16(0)
+    masses, columns = [], []
     for b in range(CAP):
-        r = spread(row, b, I16, DR // 16)
+        r = spread(row, b, I16, 8)
         q = spread(col, b, I16, 32)
         on_upper = row_iota == r
         on_lower = row_iota == r + I16(1)
-        for kind in range(2):
-            for p in range(2):
-                v = spread(parts[2 * kind][p], b, BF16, DR // 16)
-                w = spread(parts[2 * kind + 1][p], b, BF16, DR // 16)
-                lhs[pl.ds((2 * kind + p) * DR, DR), pl.ds(128 * b, 128)] = jnp.where(
-                    on_upper, v, jnp.where(on_lower, w, BF16(0))
-                )
-        hot[:, pl.ds(128 * b, 128)] = jnp.where(col_iota == q, BF16(1), BF16(0))
+        spill = jnp.zeros((16, 128), BF16)
+        block = []
+        for n in range(4):
+            kind, p = n // 2, n % 2
+            v = spread(parts[2 * kind][p], b, BF16, 8)
+            w = spread(parts[2 * kind + 1][p], b, BF16, 8)
+            block.append(jnp.where(on_upper, v, jnp.where(on_lower, w, zero)))
+            spill = jnp.where(spill_iota == I16(n), w[0:16], spill)
+        block.append(jnp.where(r[0:16] == I16(127), spill, zero))
+        masses.append(jnp.concatenate(block, axis=0))
+        columns.append(jnp.where(col_iota == q, BF16(1), zero))
     acc[...] += lax.dot_general(
-        lhs[...], hot[...], (((1,), (1,)), ((), ())), preferred_element_type=F32
+        jnp.concatenate(masses, axis=1),
+        jnp.concatenate(columns, axis=1),
+        (((1,), (1,)), ((), ())),
+        preferred_element_type=F32,
     )
 
 
@@ -136,13 +168,13 @@
     n_rows, n_cols,
     u_in, m_in, cells_in, off_in, w_in, dest_in, end_in,
     value_out, density_out,
-    um, ua, ub, grid, cells, off_raw, off, frac, w, ends, dest, corners,
+    um, ua, ub, grid, cells, off_raw, off, frac, w, ends, dest, corners, table,
     side_send, side_recv, corner_recv,
     static_send, static_recv, move_send, move_recv,
-    lhs, hot, acc,
+    acc,
     g_side_l, g_side_r, g_from_u, g_from_d, g_from_l, g_from_r, g_from_ul, g_from_ur, g_from_dl, g_from_dr,
-    red_send, red_recv, result,
-    load_sem, out_sem,
+    red_send, red_recv,
+    load_sem,
     halo_s, halo_r, static_s, static_r, move_s, move_r, g_s, g_r, red_s, red_r,
 ):
     row = lax.axis_index("rows")
@@ -173,15 +205,32 @@
     far_peers = [lax.rem(row + 8 * j, n_rows) for j in range(1, 4)]
 
     barrier = pltpu.get_barrier_semaphore()
-    greet = [at(dr, k) for dr, k in group if (dr, k) != (0, 0)]
-    greet += [(p, col) for p in row_peers + far_peers]
-    for to in greet:
-        pl.semaphore_signal(barrier, inc=1, device_id=to, device_id_type=pl.DeviceIdType.MESH)
+    has_up, has_down = row > 0, row < n_rows - 1
+    has_left, has_right = col > 0, col < n_cols - 1
+
+    def there(dr, dc=0):
+        rows_ok = {-1: has_up, 0: None, 1: has_down}[dr]
+        cols_ok = {-1: has_left, 0: None, 1: has_right}[dc]
+        if rows_ok is None or cols_ok is None:
+            return cols_ok if rows_ok is None else rows_ok
+        return rows_ok & cols_ok
+
+    def only(cond, act):
+        if cond is None:
+            act()
+        else:
+            pl.when(cond)(act)
+
+    greet = [(there(dr), at(dr, k)) for dr, k in group if (dr, k) != (0, 0)]
+    greet += [(None, (p, col)) for p in row_peers + far_peers]
+    for cond, to in greet:
+        only(cond, lambda to=to: pl.semaphore_signal(
+            barrier, inc=1, device_id=to, device_id_type=pl.DeviceIdType.MESH
+        ))
+    greeted = len(greet) - n_cols * ((1 - has_up.astype(jnp.int32)) + (1 - has_down.astype(jnp.int32)))
 
     lane = lax.broadcasted_iota(jnp.int32, (8, 128), 1)
     sub = lax.broadcasted_iota(jnp.int32, (8, 128), 0)
-    has_up, has_down = row > 0, row < n_rows - 1
-    has_left, has_right = col > 0, col < n_cols - 1
     row_in = (has_down, has_up)
     lane_right = lane < jnp.where(has_right, 8, 0)
     lane_left = lane >= jnp.where(has_left, 120, 128)
@@ -194,8 +243,9 @@
         last = um[v, 0:RT, :, 384:512].reshape(128, 128).T
         side_send[0, v] = first[0:8]
         side_send[1, v] = last[120:128]
-    pl.semaphore_wait(barrier, len(greet))
-
+    pl.semaphore_wait(barrier, greeted)
+
+    halo_to = [(-1, 0), (1, 0), (-1, -1), (-1, 1), (1, -1), (1, 1), (0, -1), (0, 1)]
     halo = [
         remote(um.at[:, 0, :, pl.ds(0, 512)], um.at[:, RT, :, pl.ds(0, 512)], halo_s.at[0], halo_r.at[0], at(-1, 0)),
         remote(um.at[:, RT - 1, :, pl.ds(0, 512)], um.at[:, RT + 1, :, pl.ds(0, 512)], halo_s.at[1], halo_r.at[1], at(1, 0)),
@@ -206,8 +256,25 @@
         remote(side_send.at[0], side_recv.at[0], halo_s.at[6], halo_r.at[6], at(0, -1)),
         remote(side_send.at[1], side_recv.at[1], halo_s.at[7], halo_r.at[7], at(0, 1)),
     ]
-    for c in halo:
-        c.start()
+    for c, to in zip(halo, halo_to):
+        only(there(*to), c.start)
+
+    def finish(copies, targets):
+        for c, (dr, dc) in zip(copies, targets):
+            only(there(dr, dc), c.wait_send)
+            only(there(-dr, -dc), c.wait_recv)
+
+    for v in range(2):
+        for s_, cond in ((2, has_up), (0, has_down)):
+
+            @pl.when(jnp.logical_not(cond))
+            def _(s_=s_, v=v):
+                missing = jnp.zeros((n_cols, 2, CAP, 128), F32)
+                if v == 0:
+                    static_recv[n_cols * s_ : n_cols * s_ + n_cols] = missing
+                for i in range(ITERS // 2):
+                    move_recv[v * (ITERS // 2) + i, n_cols * s_ : n_cols * s_ + n_cols] = missing
+
 
     loads[3].wait()
     red_send[0] = w[0] + w[1] + w[2] + w[3]
@@ -253,7 +320,7 @@
         for i, (dr, k) in enumerate(group):
             if i != SELF:
                 copies[i] = remote(send.at[i], recv.at[i], ss.at[i], rs.at[i], at(dr, k))
-                copies[i].start()
+                only(there(dr), copies[i].start)
         return copies
 
     loads[4].wait()
@@ -276,8 +343,7 @@
     for n in range(2):
         frac[n] = 0.5 + 0.45 * jnp.tanh(off[n])
 
-    for c in halo:
-        c.wait()
+    finish(halo, halo_to)
     zero_mid = jnp.zeros((112, 128), F32)
     for v in range(2):
         strip = jnp.concatenate([side_recv[0, v], zero_mid, side_recv[1, v]], axis=0).T
@@ -319,9 +385,10 @@
                 remote(grid.at[0, :, pl.ds(384, 256)], g_from_dl, ss.at[6], rs.at[6], at(-1, 1)),
                 remote(grid.at[0, :, pl.ds(0, 128)], g_from_dr, ss.at[7], rs.at[7], at(-1, -1)),
             ]
-        for c in copies:
-            c.start()
-        return copies
+        targets = [(1, 0), (0, 1), (1, 1), (-1, 0), (0, -1), (1, -1), (-1, 1), (-1, -1)][: len(copies)]
+        for c, to in zip(copies, targets):
+            only(there(*to), c.start)
+        return copies, targets
 
     def gather_edges(it):
         full = it + 1 < ITERS
@@ -376,15 +443,13 @@
         if it == 0:
             reduce_stage(0)
         else:
-            value_copy = pltpu.make_async_copy(ub.at[pl.ds(0, RT), :, pl.ds(0, 512)], value_out, out_sem.at[0])
-            value_copy.start()
-        ua[0 : RT + 1] = pltpu.roll(ub[0 : RT + 1].reshape(8 * RT + 8, 640), 639, 1).reshape(RT + 1, 8, 640)
-        sample(ub, ua, cells, corners)
-        dx0, dx1 = corners[1] - corners[0], corners[3] - corners[2]
-        dy0, dy1 = corners[2] - corners[0], corners[3] - corners[1]
+            value_out[...] = ub[0:RT, :, 0:512]
+        slopes(ub, table, lane, sub)
+        sample(table, cells, corners)
+        dx0, dx1, dy0 = corners[0], corners[1], corners[2]
         fx, fy = frac[0], frac[1]
         gx = (1.0 - fy) * dx0 + fy * dx1
-        gy = (1.0 - fx) * dy0 + fx * dy1
+        gy = (1.0 - fx) * dy0 + fx * (dy0 + (dx1 - dx0))
         hx = 0.5 + 0.45 * jnp.tanh(off[0] - gx)
         hy = 0.5 + 0.45 * jnp.tanh(off[1] - gy)
         placed = place(placing, jnp.concatenate([hx.reshape(32, 128), hy.reshape(32, 128)], axis=1))
@@ -396,45 +461,53 @@
         if it == 0:
             reduce_stage(1)
 
-        def arrivals(i, carry):
-            s = lax.rem(i + SELF, GROUP)
-
-            @pl.when(i > 0)
-            def _():
+        step = 4 * (2 * lax.rem(row, 2) - 1)
+        kinds = sum(kind * 3**i for i, (kind, _) in enumerate(ORDER))
+        dists = sum(k * 4**i for i, (_, k) in enumerate(ORDER))
+
+        def arrive(i, kinds, dists):
+            kind, k = lax.rem(kinds, 3) - 1, lax.rem(dists, 4)
+            s = SELF + kind * step + k
+            from_up, from_down = kind * step > 0, kind * step < 0
+
+            def wait():
                 remote(move_send.at[it, s], move_recv.at[it, s], move_s.at[it, s], move_r.at[it, s], at(0, 1)).wait_recv()
                 if it == 0:
                     remote(static_send.at[s], static_recv.at[s], static_s.at[s], static_r.at[s], at(0, 1)).wait_recv()
 
-            build_and_add(static_recv[s], move_recv[it, s], lhs, hot, acc)
-            return carry
-
-        lax.fori_loop(0, GROUP, arrivals, 0)
-        zero = jnp.zeros((DR, 128), F32)
-        here = acc[0:DR] + acc[DR : 2 * DR]
-        beside = acc[2 * DR : 3 * DR] + acc[3 * DR : 4 * DR]
+            absent = (from_up & (row == 0)) | (from_down & (row == n_rows - 1))
+            pl.when((i > 0) & jnp.logical_not(absent))(wait)
+            return s, kinds // 3, dists // 4
+
+        def arrivals(i, carry):
+            s, kinds, dists = arrive(i, *carry)
+            deposit(static_recv[s], move_recv[it, s], acc)
+            return kinds, dists
+
+        lax.fori_loop(0, GROUP, arrivals, (jnp.int32(kinds), jnp.int32(dists)))
+        tops = jnp.zeros((7, 512), F32)
+        here = jnp.concatenate([acc[0:128] + acc[128:256], acc[512:513] + acc[513:514], tops, jnp.zeros((8, 512), F32)], axis=0)
+        beside = jnp.concatenate([acc[256:384] + acc[384:512], acc[514:515] + acc[515:516], tops, jnp.zeros((8, 512), F32)], axis=0)
+        zero = jnp.zeros((144, 128), F32)
         whole = jnp.concatenate([here, zero], axis=1) + pltpu.roll(jnp.concatenate([beside, zero], axis=1), 1, 1)
         grid[...] = whole.reshape(RT + 2, 8, 640)
-        copies = exchange(it)
+        copies, targets = exchange(it)
         if it == 0:
             total = reduce_stage(2)
             scale = jnp.float32(n_rows * n_cols * 128 * 512) / jnp.sum(total, keepdims=True)
-        for c in list(move_copies.values()) + (list(static_copies.values()) if it == 0 else []):
-            c.wait_send()
-        for c in copies:
-            c.wait()
+        for sent in (move_copies, static_copies) if it == 0 else (move_copies,):
+            for i, c in sent.items():
+                only(there(group[i][0]), c.wait_send)
+        finish(copies, targets)
         gather_edges(it)
         if it + 1 < ITERS:
             um[1] = 0.5 * um[1] + 0.5 * (grid[...] * scale.reshape(1, 1, 1))
         else:
-            result[...] = 0.5 * um[1, 0:RT, :, 0:512] + 0.5 * (grid[0:RT, :, 0:512] * scale.reshape(1, 1, 1))
-            density_copy = pltpu.make_async_copy(result, density_out, out_sem.at[1])
-            density_copy.start()
-            value_copy.wait()
-            density_copy.wait()
+            density_out[...] = 0.5 * um[1, 0:RT, :, 0:512] + 0.5 * (grid[0:RT, :, 0:512] * scale.reshape(1, 1, 1))
 
 
 def body(n_rows, n_cols, terminal_value, density_start, start_cells, offsets, weights, dest_tiles, end_cells):
-    any_ = pl.BlockSpec(memory_space=pl.ANY)
+    any_ = pl.BlockSpec(memory_space=pltpu.HBM)
     vmem = pltpu.VMEM
     dma = pltpu.SemaphoreType.DMA
     tile = jax.ShapeDtypeStruct((RT, 8, 512), F32)
@@ -442,25 +515,25 @@
         functools.partial(kernel, n_rows, n_cols),
         out_shape=(tile, tile),
         in_specs=[any_] * 7,
-        out_specs=(any_, any_),
+        out_specs=(pl.BlockSpec(memory_space=pltpu.VMEM),) * 2,
         scratch_shapes=[
             vmem((2, RT + 2, 8, 640), F32), vmem((RT + 2, 8, 640), F32), vmem((RT + 2, 8, 640), F32),
             vmem((RT + 2, 8, 640), F32),
             vmem((4, 8, 128), jnp.int32), vmem((2, 4096), F32), vmem((2, 4, 8, 128), F32), vmem((2, 4, 8, 128), F32),
-            vmem((4, 8, 128), F32), vmem((4, 8, 128), jnp.int32), vmem((1, 32), jnp.int32), vmem((4, 4, 8, 128), F32),
+            vmem((4, 8, 128), F32), vmem((4, 8, 128), jnp.int32), vmem((1, 32), jnp.int32), vmem((3, 4, 8, 128), F32), vmem((1040, 256), BF16),
             vmem((2, 2, 8, 128), F32), vmem((2, 2, 8, 128), F32), vmem((4, 2, 8, 128), F32),
             vmem((GROUP, 2, CAP, 128), F32), vmem((GROUP, 2, CAP, 128), F32),
             vmem((ITERS, GROUP, 2, CAP, 128), F32), vmem((ITERS, GROUP, 2, CAP, 128), F32),
-            vmem((4 * DR, 1024), BF16), vmem((512, 1024), BF16), vmem((4 * DR, 512), F32),
+            vmem((528, 512), F32),
             vmem((2, 8, 128), F32), vmem((ITERS, 4, 8, 128), F32),
             vmem((ITERS, 2, 8, 640), F32), vmem((8, 640), F32), vmem((ITERS, 4, 8, 128), F32), vmem((2, 8, 128), F32),
             vmem((ITERS, 2, 8, 256), F32), vmem((2, 8, 128), F32), vmem((8, 256), F32), vmem((8, 128), F32),
-            vmem((3, 8, 128), F32), vmem((13, 8, 128), F32), vmem((RT, 8, 512), F32),
-            dma((7,)), dma((2,)),
+            vmem((3, 8, 128), F32), vmem((13, 8, 128), F32),
+            dma((7,)),
             dma((8,)), dma((8,)), dma((GROUP,)), dma((GROUP,)),
             dma((ITERS, GROUP)), dma((ITERS, GROUP)), dma((ITERS, 8)), dma((ITERS, 8)), dma((13,)), dma((13,)),
         ],
-        compiler_params=pltpu.CompilerParams(collective_id=0, has_side_effects=True),
+        compiler_params=pltpu.CompilerParams(collective_id=0, has_side_effects=True, vmem_limit_bytes=20 << 20),
         name="crowd",
     )(
         terminal_value.reshape(RT, 8, 512),

time: 68.2 us -> 58 us (0.85)
  the two profiles are of different devices: /device:TPU:1 before, /device:TPU:40 now
where the time goes in v2:
time: 58 us; the launch traced here: 57.2 us
  Pallas kernels  49.7 us (86%)
  local copies, waits for them, and re-layouts  6.86 us (12%)
  between operations  0.66 us (1%)
    pallas_call x1, Pallas kernels, body(): pl.pallas_call(functools.partial(kernel, n_rows, n_cols), out_shape=(tile...  49.7 us
    unnamed x16, local copies, waits for them, and re-layouts  6.86 us

profile of v2, /device:TPU:40, one launch (start us, length us, event | category | flops | bytes accessed | tf_op | source)
XLA Modules:
  0.0 57.2 jit_solution(7849488150626155210)
XLA Ops:
  0.6 0.0 copy-start.6
  0.6 0.6 %copy-done.6 = s32[32]{0:T(128)S(1)} copy-done((s32[32]{0:T(128)S(1)}, s32[32]{0:T(128)}, u32[]{:S(2)}) %copy-start.6) | copy-done | bytes 152
  1.3 0.0 copy-start
  1.3 0.9 %copy-done = f32[128,512]{1,0:T(8,128)S(1)} copy-done((f32[128,512]{1,0:T(8,128)S(1)}, f32[128,512]{1,0:T(8,128)}, u32[]{:S(2)}) %copy-start) | copy-done | bytes 262168
  2.2 0.0 copy-start.1
  2.2 0.9 %copy-done.1 = f32[128,512]{1,0:T(8,128)S(1)} copy-done((f32[128,512]{1,0:T(8,128)S(1)}, f32[128,512]{1,0:T(8,128)}, u32[]{:S(2)}) %copy-start.1) | copy-done | bytes 262168
  3.2 0.0 copy-start.2
  3.2 0.8 %copy-done.2 = f32[2,4096]{1,0:T(2,128)S(1)} copy-done((f32[2,4096]{1,0:T(2,128)S(1)}, f32[2,4096]{1,0:T(2,128)}, u32[]{:S(2)}) %copy-start.2) | copy-done | bytes 32792
  3.9 0.0 copy-start.3
  4.0 0.7 %copy-done.3 = s32[4096]{0:T(1024)S(1)} copy-done((s32[4096]{0:T(1024)S(1)}, s32[4096]{0:T(1024)}, u32[]{:S(2)}) %copy-start.3) | copy-done | bytes 16408
  4.7 0.0 copy-start.4
  4.7 0.7 %copy-done.4 = f32[4096]{0:T(1024)S(1)} copy-done((f32[4096]{0:T(1024)S(1)}, f32[4096]{0:T(1024)}, u32[]{:S(2)}) %copy-start.4) | copy-done | bytes 16408
  5.4 0.0 copy-start.5
  5.4 0.7 %copy-done.5 = s32[4096]{0:T(1024)S(1)} copy-done((s32[4096]{0:T(1024)S(1)}, s32[4096]{0:T(1024)}, u32[]{:S(2)}) %copy-start.5) | copy-done | bytes 16408
  6.1 49.7 %crowd.1 = (f32[16,8,512]{2,1,0:T(8,128)S(1)}, f32[16,8,512]{2,1,0:T(8,128)S(1)}) custom-call(f32[16,8,512]{2,1,0:T(8,128)S(1)} %bitcast.8, f32[16,8,512]{2,1,0:T(8,128)S(1)} %bitcast.9, s32[4,8,128]{2,1,0:T(8,128)S(1)} %bitcast.12, f32[2,4096]{1,0:T(2,128)S(1)} %copy-done.2, f32[4,8,128]{2,1,0:T(8,128)S(1)} %bitcast.13, s32[1,32]{1,0:T(1,128)S(1)} %bitcast.15, ...), custom_call_target="tpu_custom_call" | custom-call | tf_op jit(solution)/shard_map/crowd/pallas_call | solution.py:514
  55.8 0.7 %copy.11 = f32[128,512]{1,0:T(8,128)} copy(f32[128,512]{1,0:T(8,128)S(1)} %bitcast.11) | data formatting | bytes 524288
  56.5 0.7 %copy.12 = f32[128,512]{1,0:T(8,128)} copy(f32[128,512]{1,0:T(8,128)S(1)} %bitcast.10) | data formatting | bytes 524288
Async XLA Ops:
  0.6 0.7 %copy-start.6 = (s32[32]{0:T(128)S(1)}, s32[32]{0:T(128)}, u32[]{:S(2)}) copy-start(s32[32]{0:T(128)} %param.12) | copy-start | bytes 388
  1.3 0.9 %copy-start = (f32[128,512]{1,0:T(8,128)S(1)}, f32[128,512]{1,0:T(8,128)}, u32[]{:S(2)}) copy-start(f32[128,512]{1,0:T(8,128)} %param.7) | copy-start | bytes 786436
  2.2 0.9 %copy-start.1 = (f32[128,512]{1,0:T(8,128)S(1)}, f32[128,512]{1,0:T(8,128)}, u32[]{:S(2)}) copy-start(f32[128,512]{1,0:T(8,128)} %param.8) | copy-start | bytes 786436
  3.2 0.8 %copy-start.2 = (f32[2,4096]{1,0:T(2,128)S(1)}, f32[2,4096]{1,0:T(2,128)}, u32[]{:S(2)}) copy-start(f32[2,4096]{1,0:T(2,128)} %off_in.1) | copy-start | bytes 98308
  3.9 0.7 %copy-start.3 = (s32[4096]{0:T(1024)S(1)}, s32[4096]{0:T(1024)}, u32[]{:S(2)}) copy-start(s32[4096]{0:T(1024)} %param.9) | copy-start | bytes 49156
  4.7 0.7 %copy-start.4 = (f32[4096]{0:T(1024)S(1)}, f32[4096]{0:T(1024)}, u32[]{:S(2)}) copy-start(f32[4096]{0:T(1024)} %param.11) | copy-start | bytes 49156
  5.4 0.7 %copy-start.5 = (s32[4096]{0:T(1024)S(1)}, s32[4096]{0:T(1024)}, u32[]{:S(2)}) copy-start(s32[4096]{0:T(1024)} %param.13) | copy-start | bytes 49156

commit v3 on v2

--- a/solution.py
+++ b/solution.py
@@ -13,6 +13,7 @@
 RT = 16
 LT = 4
 ORDER = ((1, 0), (2, 0), (1, 1), (1, 3), (2, 1), (2, 3), (0, 0), (1, 2), (2, 2), (0, 1), (0, 3), (0, 2))
+BATCHES = ((0, 6, 2),)
 F32 = jnp.float32
 BF16 = jnp.bfloat16
 I16 = jnp.int16
@@ -120,7 +121,7 @@
     return out
 
 
-def deposit(static, moves, acc):
+def factors(static, moves, masses, columns):
     cell = static[0].astype(jnp.int32)
     mass = static[1]
     x, y = moves[0], moves[1]
@@ -139,7 +140,6 @@
         return jnp.tile(tile, (copies, 1)) if copies > 1 else tile
 
     zero = BF16(0)
-    masses, columns = [], []
     for b in range(CAP):
         r = spread(row, b, I16, 8)
         q = spread(col, b, I16, 32)
@@ -156,6 +156,12 @@
         block.append(jnp.where(r[0:16] == I16(127), spill, zero))
         masses.append(jnp.concatenate(block, axis=0))
         columns.append(jnp.where(col_iota == q, BF16(1), zero))
+
+
+def deposit(slots, acc):
+    masses, columns = [], []
+    for static, moves in slots:
+        factors(static, moves, masses, columns)
     acc[...] += lax.dot_general(
         jnp.concatenate(masses, axis=1),
         jnp.concatenate(columns, axis=1),
@@ -362,6 +368,27 @@
     def exchange(it):
         full = it + 1 < ITERS
         ss, rs = g_s.at[it], g_r.at[it]
+        sends = [
+            (grid.at[pl.ds(RT - 1, 2)], g_from_u.at[it], (1, 0)),
+            (grid.at[pl.ds(RT - 1, 2), :, pl.ds(384, 256)], g_from_ul.at[it], (1, 1)),
+        ]
+        if full:
+            sends += [
+                (grid.at[0], g_from_d, (-1, 0)),
+                (grid.at[pl.ds(RT - 1, 2), :, pl.ds(0, 128)], g_from_ur, (1, -1)),
+                (grid.at[0, :, pl.ds(384, 256)], g_from_dl, (-1, 1)),
+                (grid.at[0, :, pl.ds(0, 128)], g_from_dr, (-1, -1)),
+            ]
+        copies, targets = [], []
+
+        def send(src, dst, to):
+            n = len(copies)
+            copies.append(remote(src, dst, ss.at[n], rs.at[n], at(*to)))
+            targets.append(to)
+            only(there(*to), copies[-1].start)
+
+        for x in sends:
+            send(*x)
         third = grid[0:RT, :, 384:512].reshape(128, 128).T
         fourth = grid[0:RT, :, 512:640].reshape(128, 128).T
         g_side_r[it, 0] = third[120:128]
@@ -372,22 +399,9 @@
             first = grid[0:RT, :, 0:128].reshape(128, 128).T
             g_side_l[0] = first[0:8]
             g_side_l[1] = grid[RT, :, 0:128]
-        copies = [
-            remote(grid.at[pl.ds(RT - 1, 2)], g_from_u.at[it], ss.at[0], rs.at[0], at(1, 0)),
-            remote(g_side_r.at[it], g_from_l.at[it], ss.at[1], rs.at[1], at(0, 1)),
-            remote(grid.at[pl.ds(RT - 1, 2), :, pl.ds(384, 256)], g_from_ul.at[it], ss.at[2], rs.at[2], at(1, 1)),
-        ]
-        if full:
-            copies += [
-                remote(grid.at[0], g_from_d, ss.at[3], rs.at[3], at(-1, 0)),
-                remote(g_side_l, g_from_r, ss.at[4], rs.at[4], at(0, -1)),
-                remote(grid.at[pl.ds(RT - 1, 2), :, pl.ds(0, 128)], g_from_ur, ss.at[5], rs.at[5], at(1, -1)),
-                remote(grid.at[0, :, pl.ds(384, 256)], g_from_dl, ss.at[6], rs.at[6], at(-1, 1)),
-                remote(grid.at[0, :, pl.ds(0, 128)], g_from_dr, ss.at[7], rs.at[7], at(-1, -1)),
-            ]
-        targets = [(1, 0), (0, 1), (1, 1), (-1, 0), (0, -1), (1, -1), (-1, 1), (-1, -1)][: len(copies)]
-        for c, to in zip(copies, targets):
-            only(there(*to), c.start)
+        send(g_side_r.at[it], g_from_l.at[it], (0, 1))
+        if full:
+            send(g_side_l, g_from_r, (0, -1))
         return copies, targets
 
     def gather_edges(it):
@@ -442,8 +456,6 @@
         hjb(ua, ub, den)
         if it == 0:
             reduce_stage(0)
-        else:
-            value_out[...] = ub[0:RT, :, 0:512]
         slopes(ub, table, lane, sub)
         sample(table, cells, corners)
         dx0, dx1, dy0 = corners[0], corners[1], corners[2]
@@ -458,8 +470,8 @@
             move_recv[it, SELF, n] = placed[SELF * CAP : SELF * CAP + CAP, 128 * n : 128 * n + 128]
         move_copies = send_group(move_send.at[it], move_recv.at[it], move_s.at[it], move_r.at[it])
         acc[...] = jnp.zeros_like(acc)
-        if it == 0:
-            reduce_stage(1)
+        if it + 1 == ITERS:
+            value_out[...] = ub[0:RT, :, 0:512]
 
         step = 4 * (2 * lax.rem(row, 2) - 1)
         kinds = sum(kind * 3**i for i, (kind, _) in enumerate(ORDER))
@@ -479,12 +491,18 @@
             pl.when((i > 0) & jnp.logical_not(absent))(wait)
             return s, kinds // 3, dists // 4
 
-        def arrivals(i, carry):
-            s, kinds, dists = arrive(i, *carry)
-            deposit(static_recv[s], move_recv[it, s], acc)
-            return kinds, dists
-
-        lax.fori_loop(0, GROUP, arrivals, (jnp.int32(kinds), jnp.int32(dists)))
+        def arrivals(first, batch, i, carry):
+            slots = []
+            for j in range(batch):
+                s, *carry = arrive(first + batch * i + j, *carry)
+                slots.append((static_recv[s], move_recv[it, s]))
+            deposit(slots, acc)
+            return tuple(carry)
+
+        carry = (jnp.int32(kinds), jnp.int32(dists))
+        for first, count, batch in BATCHES:
+            step_ = functools.partial(arrivals, first, batch)
+            carry = step_(0, carry) if count == 1 else lax.fori_loop(0, count, step_, carry)
         tops = jnp.zeros((7, 512), F32)
         here = jnp.concatenate([acc[0:128] + acc[128:256], acc[512:513] + acc[513:514], tops, jnp.zeros((8, 512), F32)], axis=0)
         beside = jnp.concatenate([acc[256:384] + acc[384:512], acc[514:515] + acc[515:516], tops, jnp.zeros((8, 512), F32)], axis=0)
@@ -493,17 +511,30 @@
         grid[...] = whole.reshape(RT + 2, 8, 640)
         copies, targets = exchange(it)
         if it == 0:
-            total = reduce_stage(2)
-            scale = jnp.float32(n_rows * n_cols * 128 * 512) / jnp.sum(total, keepdims=True)
+            reduce_stage(1)
         for sent in (move_copies, static_copies) if it == 0 else (move_copies,):
             for i, c in sent.items():
                 only(there(group[i][0]), c.wait_send)
         finish(copies, targets)
+        if it == 0:
+            total = reduce_stage(2)
+            scale = jnp.float32(n_rows * n_cols * 128 * 512) / jnp.sum(total, keepdims=True)
         gather_edges(it)
         if it + 1 < ITERS:
             um[1] = 0.5 * um[1] + 0.5 * (grid[...] * scale.reshape(1, 1, 1))
         else:
             density_out[...] = 0.5 * um[1, 0:RT, :, 0:512] + 0.5 * (grid[0:RT, :, 0:512] * scale.reshape(1, 1, 1))
+
+
+def write_out(value, density, value_out, density_out, sems):
+    copies = [
+        pltpu.make_async_copy(value, value_out, sems.at[0]),
+        pltpu.make_async_copy(density, density_out, sems.at[1]),
+    ]
+    for c in copies:
+        c.start()
+    for c in copies:
+        c.wait()
 
 
 def body(n_rows, n_cols, terminal_value, density_start, start_cells, offsets, weights, dest_tiles, end_cells):
@@ -535,7 +566,7 @@
         ],
         compiler_params=pltpu.CompilerParams(collective_id=0, has_side_effects=True, vmem_limit_bytes=20 << 20),
         name="crowd",
-    )(
+    )(*(pltpu.with_memory_space_constraint(x, pltpu.HBM) for x in (
         terminal_value.reshape(RT, 8, 512),
         density_start.reshape(RT, 8, 512),
         start_cells.reshape(4, 8, 128),
@@ -543,7 +574,16 @@
         weights.reshape(4, 8, 128),
         dest_tiles.reshape(1, 32),
         end_cells.reshape(4, 8, 128),
-    )
+    )))
+    value, density = pl.pallas_call(
+        write_out,
+        out_shape=(tile, tile),
+        in_specs=[pl.BlockSpec(memory_space=pltpu.VMEM)] * 2,
+        out_specs=(pl.BlockSpec(memory_space=pltpu.HBM),) * 2,
+        scratch_shapes=[dma((2,))],
+        compiler_params=pltpu.CompilerParams(vmem_limit_bytes=1 << 20),
+        name="write_out",
+    )(value, density)
     return value.reshape(128, 512), density.reshape(128, 512)
 
 

time: 58 us -> 50 us (0.86)
  local copies, waits for them, and re-layouts: 6.86 us -> 0 us
  Pallas kernels: 49.7 us -> 48.5 us
    unnamed x16 -> x0, local copies, waits for them, and re-layouts: 6.86 us -> none
    pallas_call x1, Pallas kernels: 49.7 us -> 47.7 us  [body(): pl.pallas_call(functools.partial(kernel, n_rows, n_cols), out_shape=(tile...]
    pallas_call x0 -> x1, Pallas kernels: none -> 0.81 us  [body(): pl.pallas_call(write_out, out_shape=(tile, tile), in_specs=[pl.BlockSpec(...]
where the time goes in v3:
time: 50 us; the launch traced here: 49.2 us
  Pallas kernels  48.5 us (97%)
  between operations  0.64 us (1%)
    pallas_call x1, Pallas kernels, body(): pl.pallas_call(functools.partial(kernel, n_rows, n_cols), out_shape=(tile...  47.7 us

profile of v3, /device:TPU:40, one launch (start us, length us, event | category | flops | bytes accessed | tf_op | source)
XLA Modules:
  0.0 49.2 jit_solution(5323340784157252427)
XLA Ops:
  0.6 47.7 %crowd.1 = (f32[16,8,512]{2,1,0:T(8,128)S(1)}, f32[16,8,512]{2,1,0:T(8,128)S(1)}) custom-call(f32[16,8,512]{2,1,0:T(8,128)} %bitcast.8, f32[16,8,512]{2,1,0:T(8,128)} %bitcast.9, s32[4,8,128]{2,1,0:T(8,128)} %bitcast.10, f32[2,4096]{1,0:T(2,128)} %off_in.1, f32[4,8,128]{2,1,0:T(8,128)} %bitcast.11, s32[1,32]{1,0:T(1,128)} %bitcast.13, s32[4,8,128]{2,1,0:T(8,128)} %bitcast.12), custom_call_target="tpu_custom_call" | custom-call | tf_op jit(solution)/shard_map/crowd/pallas_call | solution.py:545
  48.4 0.8 %write_out.1 = (f32[16,8,512]{2,1,0:T(8,128)}, f32[16,8,512]{2,1,0:T(8,128)}) custom-call(f32[16,8,512]{2,1,0:T(8,128)S(1)} %get-tuple-element.6.value, f32[16,8,512]{2,1,0:T(8,128)S(1)} %get-tuple-element.7.density), custom_call_target="tpu_custom_call" | custom-call | tf_op jit(solution)/shard_map/write_out/pallas_call | solution.py:578

commit v4 on v3

--- a/solution.py
+++ b/solution.py
@@ -45,9 +45,8 @@
             right = jnp.where(lane == 127, roll(t, (j + 1) % n_j, 127, 1), roll(t, j, 127, 1))
             px = jnp.maximum(v - jnp.minimum(up, down), 0.0)
             py = jnp.maximum(v - jnp.minimum(left, right), 0.0)
-            spread = up + down + left + right - 4.0 * v
             d = den[t, :, 128 * j : 128 * j + 128]
-            new = v + 0.25 * (0.5 * spread - 0.5 * (px * px + py * py) + 0.5 * d)
+            new = 0.5 * v + 0.125 * ((up + down) + (left + right) - (px * px + py * py) + d)
             if t >= RT:
                 new = jnp.where(row_in[t - RT], new, 0.0)
             if j == LT:
@@ -55,12 +54,13 @@
             dst[t, :, 128 * j : 128 * j + 128] = new
 
 
-def slopes(u, table, lane, sub):
+def slopes(u, u1, table, lane, sub):
     def split(block, first, count):
         turned = block.T[0:count]
         high = turned.astype(BF16)
         table[pl.ds(first, count), pl.ds(0, 128)] = high
         table[pl.ds(first, count), pl.ds(128, 128)] = (turned - high.astype(F32)).astype(BF16)
+
     for j in range(LT + 1):
         js = slice(128 * j, 128 * j + 128)
         tiles = [u[t, :, js] for t in range(RT + 1)]
@@ -72,14 +72,38 @@
             for t in range(RT):
                 near = pltpu.roll(tiles[t], 127, 1)
                 far = pltpu.roll(u[t, :, 128 * j + 128 : 128 * j + 256], 127, 1)
-                dy.append(jnp.where(lane == 127, far, near) - tiles[t])
+                right = jnp.where(lane == 127, far, near)
+                u1[t, :, js] = right
+                dy.append(right - tiles[t])
             split(jnp.concatenate(dy, axis=0), 528 + 128 * j, 128)
-
-
-def sample(table, cells, corners):
-    def agents(a, carry):
+            near = pltpu.roll(tiles[RT], 127, 1)
+            far = pltpu.roll(u[RT, :, 128 * j + 128 : 128 * j + 256], 127, 1)
+            u1[RT, :, js] = jnp.where(lane == 127, far, near)
+
+
+def sample(table, u, u1, cells, corners):
+    one_cell = cells[0]
+    key, idx = one_cell >> 7, one_cell & 127
+    zero1 = jnp.zeros((8, 128), F32)
+    def agents(t, acc):
+        a = t + 1
         cell = cells[a]
         row, col = cell >> 9, cell & 511
+        u00, u10, u01, u11 = acc
+        kk = key - t * (48 * LT)
+        def look(lo, hi):
+            nonlocal u00, u10, u01, u11
+            for r in range(lo, hi):
+                for j in range(LT):
+                    part = (t * 6 + r // 8, slice(r % 8, r % 8 + 1), slice(128 * j, 128 * j + 128))
+                    here = jnp.take_along_axis(jnp.broadcast_to(u[part], (8, 128)), idx, axis=1)
+                    next_ = jnp.take_along_axis(jnp.broadcast_to(u1[part], (8, 128)), idx, axis=1)
+                    hit = kk == r * LT + j
+                    u00 = jnp.where(hit, here, u00)
+                    u01 = jnp.where(hit, next_, u01)
+                    hit = kk == (r - 1) * LT + j
+                    u10 = jnp.where(hit, here, u10)
+                    u11 = jnp.where(hit, next_, u11)
         for h in range(2):
             hot, places = [], []
             for b in range(4 * h, 4 * h + 4):
@@ -98,12 +122,16 @@
                 d1 = jnp.where(place == 8 * i - 1, x, d1)
                 e0 = jnp.where(here, picked[528 + 8 * i : 536 + 8 * i], e0)
             d1 = jnp.where(place == 511, picked[512:520], d1)
+            look(24 * h, 24 * h + 24)
             for n, v in enumerate((d0, d1, e0)):
                 v = jnp.sum(v, axis=0, keepdims=True)
                 for b in range(4):
                     corners[n, a, 4 * h + b : 4 * h + b + 1, :] = v[:, 128 * b : 128 * b + 128]
-        return carry
-    lax.fori_loop(0, 4, agents, 0)
+        return u00, u10, u01, u11
+    u00, u10, u01, u11 = lax.fori_loop(0, 3, agents, (zero1, zero1, zero1, zero1))
+    corners[0, 0] = u10 - u00
+    corners[1, 0] = u11 - u01
+    corners[2, 0] = u01 - u00
 
 
 def exact_parts(v):
@@ -368,6 +396,31 @@
     def exchange(it):
         full = it + 1 < ITERS
         ss, rs = g_s.at[it], g_r.at[it]
+        zero = jnp.zeros((8, 128), F32)
+
+        def assemble(t):
+            for j in range(LT + 1):
+                js, before = slice(128 * j, 128 * j + 128), slice(128 * j - 128, 128 * j)
+                here = beside = prior = zero
+                if t < RT:
+                    r = [slice(128 * n + 8 * t, 128 * n + 8 * t + 8) for n in range(4)]
+                    if j < LT:
+                        here = acc[r[0], js] + acc[r[1], js]
+                        beside = pltpu.roll(acc[r[2], js] + acc[r[3], js], 1, 1)
+                    if j > 0:
+                        prior = pltpu.roll(acc[r[2], before] + acc[r[3], before], 1, 1)
+                elif t == RT:
+                    if j < LT:
+                        x = acc[512:520, js]
+                        here = jnp.where(sub == 0, x + pltpu.roll(x, 7, 0), 0.0)
+                        beside = pltpu.roll(jnp.where(sub == 0, pltpu.roll(x, 6, 0) + pltpu.roll(x, 5, 0), 0.0), 1, 1)
+                    if j > 0:
+                        x = acc[512:520, before]
+                        prior = pltpu.roll(jnp.where(sub == 0, pltpu.roll(x, 6, 0) + pltpu.roll(x, 5, 0), 0.0), 1, 1)
+                grid[t, :, js] = here + jnp.where(lane == 0, prior, beside)
+
+        for t in (0, RT - 1, RT):
+            assemble(t)
         sends = [
             (grid.at[pl.ds(RT - 1, 2)], g_from_u.at[it], (1, 0)),
             (grid.at[pl.ds(RT - 1, 2), :, pl.ds(384, 256)], g_from_ul.at[it], (1, 1)),
@@ -389,6 +442,8 @@
 
         for x in sends:
             send(*x)
+        for t in list(range(1, RT - 1)) + [RT + 1]:
+            assemble(t)
         third = grid[0:RT, :, 384:512].reshape(128, 128).T
         fourth = grid[0:RT, :, 512:640].reshape(128, 128).T
         g_side_r[it, 0] = third[120:128]
@@ -456,8 +511,8 @@
         hjb(ua, ub, den)
         if it == 0:
             reduce_stage(0)
-        slopes(ub, table, lane, sub)
-        sample(table, cells, corners)
+        slopes(ub, ua, table, lane, sub)
+        sample(table, ub, ua, cells, corners)
         dx0, dx1, dy0 = corners[0], corners[1], corners[2]
         fx, fy = frac[0], frac[1]
         gx = (1.0 - fy) * dx0 + fy * dx1
@@ -503,12 +558,6 @@
         for first, count, batch in BATCHES:
             step_ = functools.partial(arrivals, first, batch)
             carry = step_(0, carry) if count == 1 else lax.fori_loop(0, count, step_, carry)
-        tops = jnp.zeros((7, 512), F32)
-        here = jnp.concatenate([acc[0:128] + acc[128:256], acc[512:513] + acc[513:514], tops, jnp.zeros((8, 512), F32)], axis=0)
-        beside = jnp.concatenate([acc[256:384] + acc[384:512], acc[514:515] + acc[515:516], tops, jnp.zeros((8, 512), F32)], axis=0)
-        zero = jnp.zeros((144, 128), F32)
-        whole = jnp.concatenate([here, zero], axis=1) + pltpu.roll(jnp.concatenate([beside, zero], axis=1), 1, 1)
-        grid[...] = whole.reshape(RT + 2, 8, 640)
         copies, targets = exchange(it)
         if it == 0:
             reduce_stage(1)

time: 50 us -> 48.9 us (0.978)
  Pallas kernels: 48.5 us -> 47.5 us
    pallas_call x1, Pallas kernels: 47.7 us -> 46.7 us  [body(): pl.pallas_call(functools.partial(kernel, n_rows, n_cols), out_shape=(tile...]
where the time goes in v4:
time: 48.9 us; the launch traced here: 48.1 us
  Pallas kernels  47.5 us (97%)
  between operations  0.64 us (1%)
    pallas_call x1, Pallas kernels, body(): pl.pallas_call(functools.partial(kernel, n_rows, n_cols), out_shape=(tile...  46.7 us

profile of v4, /device:TPU:40, one launch (start us, length us, event | category | flops | bytes accessed | tf_op | source)
XLA Modules:
  0.0 48.1 jit_solution(14014007978529012769)
XLA Ops:
  0.6 46.7 %crowd.1 = (f32[16,8,512]{2,1,0:T(8,128)S(1)}, f32[16,8,512]{2,1,0:T(8,128)S(1)}) custom-call(f32[16,8,512]{2,1,0:T(8,128)} %bitcast.8, f32[16,8,512]{2,1,0:T(8,128)} %bitcast.9, s32[4,8,128]{2,1,0:T(8,128)} %bitcast.10, f32[2,4096]{1,0:T(2,128)} %off_in.1, f32[4,8,128]{2,1,0:T(8,128)} %bitcast.11, s32[1,32]{1,0:T(1,128)} %bitcast.13, s32[4,8,128]{2,1,0:T(8,128)} %bitcast.12), custom_call_target="tpu_custom_call" | custom-call | tf_op jit(solution)/shard_map/crowd/pallas_call | solution.py:594
  47.3 0.8 %write_out.1 = (f32[16,8,512]{2,1,0:T(8,128)}, f32[16,8,512]{2,1,0:T(8,128)}) custom-call(f32[16,8,512]{2,1,0:T(8,128)S(1)} %get-tuple-element.6.value, f32[16,8,512]{2,1,0:T(8,128)S(1)} %get-tuple-element.7.density), custom_call_target="tpu_custom_call" | custom-call | tf_op jit(solution)/shard_map/write_out/pallas_call | solution.py:627

commit v5 on v4

--- a/solution.py
+++ b/solution.py
@@ -13,7 +13,7 @@
 RT = 16
 LT = 4
 ORDER = ((1, 0), (2, 0), (1, 1), (1, 3), (2, 1), (2, 3), (0, 0), (1, 2), (2, 2), (0, 1), (0, 3), (0, 2))
-BATCHES = ((0, 6, 2),)
+BATCHES = (((0, 3, 2), (6, 3, 2)), ((0, 6, 2),))
 F32 = jnp.float32
 BF16 = jnp.bfloat16
 I16 = jnp.int16
@@ -198,78 +198,80 @@
     )
 
 
-def kernel(
+class Place:
+    def __init__(self, n_rows, n_cols):
+        self.n_rows, self.n_cols = n_rows, n_cols
+        self.row, self.col = lax.axis_index("rows"), lax.axis_index("cols")
+        self.has_up, self.has_down = self.row > 0, self.row < n_rows - 1
+        self.has_left, self.has_right = self.col > 0, self.col < n_cols - 1
+        self.lane = lax.broadcasted_iota(jnp.int32, (8, 128), 1)
+        self.sub = lax.broadcasted_iota(jnp.int32, (8, 128), 0)
+        self.lane_right = self.lane < jnp.where(self.has_right, 8, 0)
+        self.lane_left = self.lane >= jnp.where(self.has_left, 120, 128)
+        self.side_in = self.lane_right | self.lane_left
+
+    def at(self, dr, dc):
+        n_rows, n_cols = self.n_rows, self.n_cols
+        return (lax.rem(self.row + dr + n_rows, n_rows), lax.rem(self.col + dc + n_cols, n_cols))
+
+    def there(self, dr, dc=0):
+        rows_ok = {-1: self.has_up, 0: None, 1: self.has_down}[dr]
+        cols_ok = {-1: self.has_left, 0: None, 1: self.has_right}[dc]
+        if rows_ok is None or cols_ok is None:
+            return cols_ok if rows_ok is None else rows_ok
+        return rows_ok & cols_ok
+
+    def greet(self, peers):
+        barrier = pltpu.get_barrier_semaphore()
+        count = jnp.int32(0)
+        for cond, to in peers:
+            only(cond, lambda to=to: pl.semaphore_signal(
+                barrier, inc=1, device_id=to, device_id_type=pl.DeviceIdType.MESH
+            ))
+            count = count + (1 if cond is None else cond.astype(jnp.int32))
+        return barrier, count
+
+    def finish(self, copies, targets):
+        for c, (dr, dc) in zip(copies, targets):
+            only(self.there(dr, dc), c.wait_send)
+            only(self.there(-dr, -dc), c.wait_recv)
+
+
+def only(cond, act):
+    if cond is None:
+        act()
+    else:
+        pl.when(cond)(act)
+
+
+def remote(src, dst, s, r, to):
+    return pltpu.make_async_remote_copy(
+        src_ref=src, dst_ref=dst, send_sem=s, recv_sem=r,
+        device_id=to, device_id_type=pl.DeviceIdType.MESH,
+    )
+
+
+def halo_kernel(
     n_rows, n_cols,
-    u_in, m_in, cells_in, off_in, w_in, dest_in, end_in,
-    value_out, density_out,
-    um, ua, ub, grid, cells, off_raw, off, frac, w, ends, dest, corners, table,
-    side_send, side_recv, corner_recv,
-    static_send, static_recv, move_send, move_recv,
-    acc,
-    g_side_l, g_side_r, g_from_u, g_from_d, g_from_l, g_from_r, g_from_ul, g_from_ur, g_from_dl, g_from_dr,
-    red_send, red_recv,
-    load_sem,
-    halo_s, halo_r, static_s, static_r, move_s, move_r, g_s, g_r, red_s, red_r,
+    u_in, m_in, off_in, w_in, dest_in, end_in,
+    um, off, frac, static_send, placing_out, mass_out,
+    off_raw, w, ends, dest, side_send, side_recv, corner_recv,
+    load_sem, halo_s, halo_r,
 ):
-    row = lax.axis_index("rows")
-    col = lax.axis_index("cols")
-
-    def at(dr, dc):
-        return (lax.rem(row + dr + n_rows, n_rows), lax.rem(col + dc + n_cols, n_cols))
-
-    def remote(src, dst, s, r, to):
-        return pltpu.make_async_remote_copy(
-            src_ref=src, dst_ref=dst, send_sem=s, recv_sem=r,
-            device_id=to, device_id_type=pl.DeviceIdType.MESH,
-        )
-
+    at_ = Place(n_rows, n_cols)
+    at, there, lane = at_.at, at_.there, at_.lane
+    row, col, side_in = at_.row, at_.col, at_.side_in
+    has_up, has_down = at_.has_up, at_.has_down
     loads = [
         (u_in, um.at[0, pl.ds(0, RT), :, pl.ds(0, 512)]),
         (m_in, um.at[1, pl.ds(0, RT), :, pl.ds(0, 512)]),
-        (dest_in, dest), (w_in, w), (end_in, ends), (off_in, off_raw), (cells_in, cells),
+        (dest_in, dest), (w_in, w), (end_in, ends), (off_in, off_raw),
     ]
     loads = [pltpu.make_async_copy(a, b, load_sem.at[i]) for i, (a, b) in enumerate(loads)]
     for c in loads:
         c.start()
-
-    group = [(dr, k) for dr in (-1, 0, 1) for k in range(n_cols)]
-    near = row % 8
-    base = row - near
-    row_peers = [base + (near + j) % 8 for j in range(1, 8)]
-    far_peers = [lax.rem(row + 8 * j, n_rows) for j in range(1, 4)]
-
-    barrier = pltpu.get_barrier_semaphore()
-    has_up, has_down = row > 0, row < n_rows - 1
-    has_left, has_right = col > 0, col < n_cols - 1
-
-    def there(dr, dc=0):
-        rows_ok = {-1: has_up, 0: None, 1: has_down}[dr]
-        cols_ok = {-1: has_left, 0: None, 1: has_right}[dc]
-        if rows_ok is None or cols_ok is None:
-            return cols_ok if rows_ok is None else rows_ok
-        return rows_ok & cols_ok
-
-    def only(cond, act):
-        if cond is None:
-            act()
-        else:
-            pl.when(cond)(act)
-
-    greet = [(there(dr), at(dr, k)) for dr, k in group if (dr, k) != (0, 0)]
-    greet += [(None, (p, col)) for p in row_peers + far_peers]
-    for cond, to in greet:
-        only(cond, lambda to=to: pl.semaphore_signal(
-            barrier, inc=1, device_id=to, device_id_type=pl.DeviceIdType.MESH
-        ))
-    greeted = len(greet) - n_cols * ((1 - has_up.astype(jnp.int32)) + (1 - has_down.astype(jnp.int32)))
-
-    lane = lax.broadcasted_iota(jnp.int32, (8, 128), 1)
-    sub = lax.broadcasted_iota(jnp.int32, (8, 128), 0)
-    row_in = (has_down, has_up)
-    lane_right = lane < jnp.where(has_right, 8, 0)
-    lane_left = lane >= jnp.where(has_left, 120, 128)
-    side_in = lane_right | lane_left
-
+    halo_to = [(-1, 0), (1, 0), (-1, -1), (-1, 1), (1, -1), (1, 1), (0, -1), (0, 1)]
+    barrier, greeted = at_.greet([(there(*to), at(*to)) for to in halo_to])
     for c in loads[:2]:
         c.wait()
     for v in range(2):
@@ -279,7 +281,6 @@
         side_send[1, v] = last[120:128]
     pl.semaphore_wait(barrier, greeted)
 
-    halo_to = [(-1, 0), (1, 0), (-1, -1), (-1, 1), (1, -1), (1, 1), (0, -1), (0, 1)]
     halo = [
         remote(um.at[:, 0, :, pl.ds(0, 512)], um.at[:, RT, :, pl.ds(0, 512)], halo_s.at[0], halo_r.at[0], at(-1, 0)),
         remote(um.at[:, RT - 1, :, pl.ds(0, 512)], um.at[:, RT + 1, :, pl.ds(0, 512)], halo_s.at[1], halo_r.at[1], at(1, 0)),
@@ -293,50 +294,8 @@
     for c, to in zip(halo, halo_to):
         only(there(*to), c.start)
 
-    def finish(copies, targets):
-        for c, (dr, dc) in zip(copies, targets):
-            only(there(dr, dc), c.wait_send)
-            only(there(-dr, -dc), c.wait_recv)
-
-    for v in range(2):
-        for s_, cond in ((2, has_up), (0, has_down)):
-
-            @pl.when(jnp.logical_not(cond))
-            def _(s_=s_, v=v):
-                missing = jnp.zeros((n_cols, 2, CAP, 128), F32)
-                if v == 0:
-                    static_recv[n_cols * s_ : n_cols * s_ + n_cols] = missing
-                for i in range(ITERS // 2):
-                    move_recv[v * (ITERS // 2) + i, n_cols * s_ : n_cols * s_ + n_cols] = missing
-
-
     loads[3].wait()
-    red_send[0] = w[0] + w[1] + w[2] + w[3]
-    stages = [
-        [(0, at(0, k)) for k in range(1, n_cols)],
-        [(1, (p, col)) for p in row_peers],
-        [(2, (p, col)) for p in far_peers],
-    ]
-    red, count = [], 0
-    for stage in stages:
-        copies = []
-        for s, to in stage:
-            copies.append(remote(red_send.at[s], red_recv.at[count], red_s.at[count], red_r.at[count], to))
-            count += 1
-        red.append(copies)
-    for c in red[0]:
-        c.start()
-
-    def reduce_stage(s):
-        total, first = red_send[s], sum(len(x) for x in red[:s])
-        for i, c in enumerate(red[s]):
-            c.wait()
-            total = total + red_recv[first + i]
-        if s + 1 < len(red):
-            red_send[s + 1] = total
-            for c in red[s + 1]:
-                c.start()
-        return total
+    mass_out[...] = w[0] + w[1] + w[2] + w[3]
 
     loads[2].wait()
     d = dest[...]
@@ -348,14 +307,7 @@
     slot = ((d >> 2) - row + 1) * (n_cols * CAP) + (((d & 3) - col) & 3) * CAP + rank
     slot_iota = lax.broadcasted_iota(jnp.int32, (GROUP * CAP, 32), 0)
     placing = jnp.where(slot_iota == slot, 1.0, 0.0).astype(BF16)
-
-    def send_group(send, recv, ss, rs):
-        copies = {}
-        for i, (dr, k) in enumerate(group):
-            if i != SELF:
-                copies[i] = remote(send.at[i], recv.at[i], ss.at[i], rs.at[i], at(dr, k))
-                only(there(dr), copies[i].start)
-        return copies
+    placing_out[...] = placing
 
     loads[4].wait()
     block_static = jnp.concatenate(
@@ -364,12 +316,7 @@
     placed = place(placing, block_static)
     for n in range(2):
         static_send[:, n] = placed[:, 128 * n : 128 * n + 128].reshape(GROUP, CAP, 128)
-    for n in range(2):
-        static_recv[SELF, n] = placed[SELF * CAP : SELF * CAP + CAP, 128 * n : 128 * n + 128]
-    static_copies = send_group(static_send, static_recv, static_s, static_r)
-
     loads[5].wait()
-    loads[6].wait()
     for b in range(32):
         both = off_raw[:, 128 * b : 128 * b + 128]
         for n in range(2):
@@ -377,7 +324,7 @@
     for n in range(2):
         frac[n] = 0.5 + 0.45 * jnp.tanh(off[n])
 
-    finish(halo, halo_to)
+    at_.finish(halo, halo_to)
     zero_mid = jnp.zeros((112, 128), F32)
     for v in range(2):
         strip = jnp.concatenate([side_recv[0, v], zero_mid, side_recv[1, v]], axis=0).T
@@ -392,6 +339,85 @@
             um[0, RT + 1, :, 0:512] = jnp.where(has_up, um[0, RT + 1, :, 0:512], 0.0)
         um[v, RT, :, 512:640] = below
         um[v, RT + 1, :, 512:640] = above
+
+
+def kernel(
+    n_rows, n_cols,
+    um, off, frac, static_send, placing_in, mass_in, cells_in,
+    value_out, density_out,
+    ua, ub, grid, relaxed, cells, corners, table,
+    static_recv, move_send, move_recv,
+    acc,
+    g_side_l, g_side_r, g_from_u, g_from_d, g_from_l, g_from_r, g_from_ul, g_from_ur, g_from_dl, g_from_dr,
+    red_send, red_recv,
+    load_sem,
+    static_s, static_r, move_s, move_r, g_s, g_r, red_s, red_r,
+):
+    at_ = Place(n_rows, n_cols)
+    at, there, finish, lane, sub = at_.at, at_.there, at_.finish, at_.lane, at_.sub
+    row, col, side_in = at_.row, at_.col, at_.side_in
+    has_up, has_down, has_left, has_right = at_.has_up, at_.has_down, at_.has_left, at_.has_right
+    lane_right, lane_left = at_.lane_right, at_.lane_left
+    row_in = (has_down, has_up)
+    load = pltpu.make_async_copy(cells_in, cells, load_sem.at[0])
+    load.start()
+
+    group = [(dr, k) for dr in (-1, 0, 1) for k in range(n_cols)]
+    near = row % 8
+    base = row - near
+    row_peers = [base + (near + j) % 8 for j in range(1, 8)]
+    far_peers = [lax.rem(row + 8 * j, n_rows) for j in range(1, 4)]
+    barrier, greeted = at_.greet(
+        [(there(dr), at(dr, k)) for dr, k in group if (dr, k) != (0, 0)]
+        + [(None, (p, col)) for p in row_peers + far_peers]
+    )
+    placing = placing_in[...]
+    zero_mid = jnp.zeros((112, 128), F32)
+
+    for v in range(2):
+        for s_, cond in ((2, has_up), (0, has_down)):
+
+            @pl.when(jnp.logical_not(cond))
+            def _(s_=s_, v=v):
+                missing = jnp.zeros((n_cols, 2, CAP, 128), F32)
+                if v == 0:
+                    static_recv[n_cols * s_ : n_cols * s_ + n_cols] = missing
+                for i in range(ITERS // 2):
+                    move_recv[v * (ITERS // 2) + i, n_cols * s_ : n_cols * s_ + n_cols] = missing
+    for n in range(2):
+        static_recv[SELF, n] = static_send[SELF, n]
+
+    red_send[0] = mass_in[...]
+    stages = [
+        [(0, at(0, k)) for k in range(1, n_cols)],
+        [(1, (p, col)) for p in row_peers],
+        [(2, (p, col)) for p in far_peers],
+    ]
+    red, count = [], 0
+    for stage in stages:
+        copies = []
+        for s, to in stage:
+            copies.append(remote(red_send.at[s], red_recv.at[count], red_s.at[count], red_r.at[count], to))
+            count += 1
+        red.append(copies)
+    def reduce_stage(s):
+        total, first = red_send[s], sum(len(x) for x in red[:s])
+        for i, c in enumerate(red[s]):
+            c.wait()
+            total = total + red_recv[first + i]
+        if s + 1 < len(red):
+            red_send[s + 1] = total
+            for c in red[s + 1]:
+                c.start()
+        return total
+
+    def send_group(send, recv, ss, rs):
+        copies = {}
+        for i, (dr, k) in enumerate(group):
+            if i != SELF:
+                copies[i] = remote(send.at[i], recv.at[i], ss.at[i], rs.at[i], at(dr, k))
+                only(there(dr), copies[i].start)
+        return copies
 
     def exchange(it):
         full = it + 1 < ITERS
@@ -504,15 +530,20 @@
     scale = None
     for it in range(ITERS):
         hjb = functools.partial(hjb_step, lane=lane, sub=sub, row_in=row_in, side_in=side_in)
-        den = um.at[1]
+        den = um.at[1] if it == 0 else relaxed
         hjb(um.at[0], ua, den)
         hjb(ua, ub, den)
         hjb(ub, ua, den)
         hjb(ua, ub, den)
         if it == 0:
-            reduce_stage(0)
+            load.wait()
         slopes(ub, ua, table, lane, sub)
         sample(table, ub, ua, cells, corners)
+        if it == 0:
+            pl.semaphore_wait(barrier, greeted)
+            static_copies = send_group(static_send, static_recv, static_s, static_r)
+            for c in red[0]:
+                c.start()
         dx0, dx1, dy0 = corners[0], corners[1], corners[2]
         fx, fy = frac[0], frac[1]
         gx = (1.0 - fy) * dx0 + fy * dx1
@@ -555,9 +586,10 @@
             return tuple(carry)
 
         carry = (jnp.int32(kinds), jnp.int32(dists))
-        for first, count, batch in BATCHES:
-            step_ = functools.partial(arrivals, first, batch)
-            carry = step_(0, carry) if count == 1 else lax.fori_loop(0, count, step_, carry)
+        for n, (first, count, batch) in enumerate(BATCHES[it]):
+            if n > 0:
+                reduce_stage(0)
+            carry = lax.fori_loop(0, count, functools.partial(arrivals, first, batch), carry)
         copies, targets = exchange(it)
         if it == 0:
             reduce_stage(1)
@@ -570,9 +602,9 @@
             scale = jnp.float32(n_rows * n_cols * 128 * 512) / jnp.sum(total, keepdims=True)
         gather_edges(it)
         if it + 1 < ITERS:
-            um[1] = 0.5 * um[1] + 0.5 * (grid[...] * scale.reshape(1, 1, 1))
+            relaxed[...] = 0.5 * um[1] + 0.5 * (grid[...] * scale.reshape(1, 1, 1))
         else:
-            density_out[...] = 0.5 * um[1, 0:RT, :, 0:512] + 0.5 * (grid[0:RT, :, 0:512] * scale.reshape(1, 1, 1))
+            density_out[...] = 0.5 * relaxed[0:RT, :, 0:512] + 0.5 * (grid[0:RT, :, 0:512] * scale.reshape(1, 1, 1))
 
 
 def write_out(value, density, value_out, density_out, sems):
@@ -591,39 +623,53 @@
     vmem = pltpu.VMEM
     dma = pltpu.SemaphoreType.DMA
     tile = jax.ShapeDtypeStruct((RT, 8, 512), F32)
+    whole = pl.BlockSpec(memory_space=pltpu.VMEM)
+    stay = lambda x: pltpu.with_memory_space_constraint(x, pltpu.HBM)
+    shape = jax.ShapeDtypeStruct
+    prepared = pl.pallas_call(
+        functools.partial(halo_kernel, n_rows, n_cols),
+        out_shape=(
+            shape((2, RT + 2, 8, 640), F32), shape((2, 4, 8, 128), F32), shape((2, 4, 8, 128), F32),
+            shape((GROUP, 2, CAP, 128), F32), shape((GROUP * CAP, 32), BF16), shape((8, 128), F32),
+        ),
+        in_specs=[any_] * 6,
+        out_specs=(whole,) * 6,
+        scratch_shapes=[
+            vmem((2, 4096), F32), vmem((4, 8, 128), F32), vmem((4, 8, 128), jnp.int32), vmem((1, 32), jnp.int32),
+            vmem((2, 2, 8, 128), F32), vmem((2, 2, 8, 128), F32), vmem((4, 2, 8, 128), F32),
+            dma((6,)), dma((8,)), dma((8,)),
+        ],
+        compiler_params=pltpu.CompilerParams(collective_id=1, has_side_effects=True, vmem_limit_bytes=8 << 20),
+        name="halos",
+    )(
+        stay(terminal_value.reshape(RT, 8, 512)),
+        stay(density_start.reshape(RT, 8, 512)),
+        stay(offsets),
+        stay(weights.reshape(4, 8, 128)),
+        stay(dest_tiles.reshape(1, 32)),
+        stay(end_cells.reshape(4, 8, 128)),
+    )
     value, density = pl.pallas_call(
         functools.partial(kernel, n_rows, n_cols),
         out_shape=(tile, tile),
-        in_specs=[any_] * 7,
-        out_specs=(pl.BlockSpec(memory_space=pltpu.VMEM),) * 2,
+        in_specs=[whole] * 6 + [any_],
+        out_specs=(whole, whole),
         scratch_shapes=[
-            vmem((2, RT + 2, 8, 640), F32), vmem((RT + 2, 8, 640), F32), vmem((RT + 2, 8, 640), F32),
-            vmem((RT + 2, 8, 640), F32),
-            vmem((4, 8, 128), jnp.int32), vmem((2, 4096), F32), vmem((2, 4, 8, 128), F32), vmem((2, 4, 8, 128), F32),
-            vmem((4, 8, 128), F32), vmem((4, 8, 128), jnp.int32), vmem((1, 32), jnp.int32), vmem((3, 4, 8, 128), F32), vmem((1040, 256), BF16),
-            vmem((2, 2, 8, 128), F32), vmem((2, 2, 8, 128), F32), vmem((4, 2, 8, 128), F32),
-            vmem((GROUP, 2, CAP, 128), F32), vmem((GROUP, 2, CAP, 128), F32),
-            vmem((ITERS, GROUP, 2, CAP, 128), F32), vmem((ITERS, GROUP, 2, CAP, 128), F32),
+            vmem((RT + 2, 8, 640), F32), vmem((RT + 2, 8, 640), F32), vmem((RT + 2, 8, 640), F32), vmem((RT + 2, 8, 640), F32),
+            vmem((4, 8, 128), jnp.int32), vmem((3, 4, 8, 128), F32), vmem((1040, 256), BF16),
+            vmem((GROUP, 2, CAP, 128), F32), vmem((ITERS, GROUP, 2, CAP, 128), F32), vmem((ITERS, GROUP, 2, CAP, 128), F32),
             vmem((528, 512), F32),
             vmem((2, 8, 128), F32), vmem((ITERS, 4, 8, 128), F32),
             vmem((ITERS, 2, 8, 640), F32), vmem((8, 640), F32), vmem((ITERS, 4, 8, 128), F32), vmem((2, 8, 128), F32),
             vmem((ITERS, 2, 8, 256), F32), vmem((2, 8, 128), F32), vmem((8, 256), F32), vmem((8, 128), F32),
             vmem((3, 8, 128), F32), vmem((13, 8, 128), F32),
-            dma((7,)),
-            dma((8,)), dma((8,)), dma((GROUP,)), dma((GROUP,)),
+            dma((1,)),
+            dma((GROUP,)), dma((GROUP,)),
             dma((ITERS, GROUP)), dma((ITERS, GROUP)), dma((ITERS, 8)), dma((ITERS, 8)), dma((13,)), dma((13,)),
         ],
         compiler_params=pltpu.CompilerParams(collective_id=0, has_side_effects=True, vmem_limit_bytes=20 << 20),
         name="crowd",
-    )(*(pltpu.with_memory_space_constraint(x, pltpu.HBM) for x in (
-        terminal_value.reshape(RT, 8, 512),
-        density_start.reshape(RT, 8, 512),
-        start_cells.reshape(4, 8, 128),
-        offsets,
-        weights.reshape(4, 8, 128),
-        dest_tiles.reshape(1, 32),
-        end_cells.reshape(4, 8, 128),
-    )))
+    )(*prepared, stay(start_cells.reshape(4, 8, 128)))
     value, density = pl.pallas_call(
         write_out,
         out_shape=(tile, tile),

time: 48.9 us -> 48.6 us (level)
    pallas_call x0 -> x1, Pallas kernels: none -> 8.38 us  [body(): pl.pallas_call(functools.partial(halo_kernel, n_rows, n_cols), out_shape=...]
    pallas_call x1, Pallas kernels: 46.7 us -> 38.3 us  [body(): pl.pallas_call(functools.partial(kernel, n_rows, n_cols), out_shape=(tile...]
where the time goes in v5:
time: 48.6 us; the launch traced here: 48.2 us
  Pallas kernels  47.5 us (98%)
  between operations  0.65 us (1%)
    pallas_call x1, Pallas kernels, body(): pl.pallas_call(functools.partial(kernel, n_rows, n_cols), out_shape=(tile...  38.3 us
    pallas_call x1, Pallas kernels, body(): pl.pallas_call(functools.partial(halo_kernel, n_rows, n_cols), out_shape=...  8.38 us

profile of v5, /device:TPU:40, one launch (start us, length us, event | category | flops | bytes accessed | tf_op | source)
XLA Modules:
  0.0 48.2 jit_solution(8033894469859934269)
XLA Ops:
  0.6 8.4 %halos.1 = (f32[2,18,8,640]{3,2,1,0:T(8,128)S(1)}, f32[2,4,8,128]{3,2,1,0:T(8,128)S(1)}, f32[2,4,8,128]{3,2,1,0:T(8,128)S(1)}, f32[12,2,8,128]{3,2,1,0:T(8,128)S...) custom-call(f32[16,8,512]{2,1,0:T(8,128)} %bitcast.8, f32[16,8,512]{2,1,0:T(8,128)} %bitcast.9, f32[2,4096]{1,0:T(2,128)} %off_in.1, ...), custom_call_target="tpu_custom_call" | custom-call | tf_op jit(solution)/shard_map/halos/pallas_call | solution.py:629
  9.0 38.3 %crowd.1 = (f32[16,8,512]{2,1,0:T(8,128)S(1)}, f32[16,8,512]{2,1,0:T(8,128)S(1)}) custom-call(f32[2,18,8,640]{3,2,1,0:T(8,128)S(1)} %get-tuple-element.12.um, f32[2,4,8,128]{3,2,1,0:T(8,128)S(1)} %get-tuple-element.13.off, f32[2,4,8,128]{3,2,1,0:T(8,128)S(1)} %get-tuple-element.14.frac, f32[12,2,8,128]{3,2,1,0:T(8,128)S(1)} %get-tuple-element.15.static_send, ...), custom_call_target="tpu_custom_call" | custom-call | tf_op jit(solution)/shard_map/crowd/pallas_call | solution.py:652
  47.4 0.8 %write_out.1 = (f32[16,8,512]{2,1,0:T(8,128)}, f32[16,8,512]{2,1,0:T(8,128)}) custom-call(f32[16,8,512]{2,1,0:T(8,128)S(1)} %get-tuple-element.18.value, f32[16,8,512]{2,1,0:T(8,128)S(1)} %get-tuple-element.19.density), custom_call_target="tpu_custom_call" | custom-call | tf_op jit(solution)/shard_map/write_out/pallas_call | solution.py:673

commit v6 on v5

--- a/solution.py
+++ b/solution.py
@@ -348,7 +348,7 @@
     ua, ub, grid, relaxed, cells, corners, table,
     static_recv, move_send, move_recv,
     acc,
-    g_side_l, g_side_r, g_from_u, g_from_d, g_from_l, g_from_r, g_from_ul, g_from_ur, g_from_dl, g_from_dr,
+    g_side_l, g_side_r, g_down, g_from_u, g_from_d, g_from_l, g_from_r, g_from_ul, g_from_ur, g_from_dl, g_from_dr,
     red_send, red_recv,
     load_sem,
     static_s, static_r, move_s, move_r, g_s, g_r, red_s, red_r,
@@ -447,14 +447,17 @@
 
         for t in (0, RT - 1, RT):
             assemble(t)
+        for j in range(LT + 1):
+            js = slice(128 * j, 128 * j + 128)
+            g_down[it, :, js] = jnp.where(sub == 0, grid[RT, :, js], grid[RT - 1, :, js])
         sends = [
-            (grid.at[pl.ds(RT - 1, 2)], g_from_u.at[it], (1, 0)),
-            (grid.at[pl.ds(RT - 1, 2), :, pl.ds(384, 256)], g_from_ul.at[it], (1, 1)),
+            (g_down.at[it], g_from_u.at[it], (1, 0)),
+            (g_down.at[it, :, pl.ds(384, 256)], g_from_ul.at[it], (1, 1)),
         ]
         if full:
             sends += [
                 (grid.at[0], g_from_d, (-1, 0)),
-                (grid.at[pl.ds(RT - 1, 2), :, pl.ds(0, 128)], g_from_ur, (1, -1)),
+                (g_down.at[it, :, pl.ds(0, 128)], g_from_ur, (1, -1)),
                 (grid.at[0, :, pl.ds(384, 256)], g_from_dl, (-1, 1)),
                 (grid.at[0, :, pl.ds(0, 128)], g_from_dr, (-1, -1)),
             ]
@@ -490,10 +493,12 @@
         top = sub == 0
         left0 = (lane == 0) & has_left
         l4, z = slice(512, 640), 0.0
-        grid[RT + 1] = jnp.where(has_up, g_from_u[it, 0], z)
+        above = (sub > 0) & has_up
         for j in range(LT + 1):
             js = slice(128 * j, 128 * j + 128)
-            grid[0, :, js] += jnp.where(top & has_up, g_from_u[it, 1, :, js], z)
+            grid[0, :, js] += jnp.where(top & has_up, g_from_u[it, :, js], z)
+            if full:
+                grid[RT + 1, :, js] = jnp.where(above, g_from_u[it, :, js], z)
         if full:
             grid[RT] += jnp.where(has_down, g_from_d[...], z)
         right_rows = g_from_r[0] if full else jnp.zeros((8, 128), F32)
@@ -506,15 +511,13 @@
             edge = edge + jnp.where(lane_right, g_from_r[1], z)
         grid[RT, :, l4] += edge
         grid[RT, :, 0:128] += jnp.where(left0, g_from_l[it, 3], z)
-        corner = jnp.where(lane_left, g_from_ul[it, 0, :, 0:128], z)
-        corner_top = jnp.where(lane_left, g_from_ul[it, 1, :, 0:128], z)
+        corner = jnp.where(lane_left, g_from_ul[it, :, 0:128], z)
         if full:
-            corner = corner + jnp.where(lane_right, g_from_ur[0], z)
-            corner_top = corner_top + jnp.where(lane_right, g_from_ur[1], z)
-        grid[RT + 1, :, l4] += jnp.where(has_up, corner, z)
-        grid[RT + 1, :, 0:128] += jnp.where(left0 & has_up, g_from_ul[it, 0, :, 128:256], z)
-        grid[0, :, l4] += jnp.where(top & has_up, corner_top, z)
-        grid[0, :, 0:128] += jnp.where(top & left0 & has_up, g_from_ul[it, 1, :, 128:256], z)
+            corner = corner + jnp.where(lane_right, g_from_ur[...], z)
+            grid[RT + 1, :, l4] += jnp.where(above, corner, z)
+            grid[RT + 1, :, 0:128] += jnp.where(left0 & above, g_from_ul[it, :, 128:256], z)
+        grid[0, :, l4] += jnp.where(top & has_up, corner, z)
+        grid[0, :, 0:128] += jnp.where(top & left0 & has_up, g_from_ul[it, :, 128:256], z)
         if full:
             corner = jnp.where(lane_left, g_from_dl[:, 0:128], z) + jnp.where(lane_right, g_from_dr[...], z)
             grid[RT, :, l4] += jnp.where(has_down, corner, z)
@@ -523,7 +526,7 @@
             js = slice(128 * j, 128 * j + 128)
             folded = pltpu.roll(grid[RT, :, js], 7, 0)
             grid[RT - 1, :, js] += jnp.where((sub == 7) & jnp.logical_not(has_down), folded, z)
-        for t in range(RT + 2):
+        for t in range(RT + 2 if full else RT):
             folded = pltpu.roll(grid[t, :, l4], 127, 1)
             grid[t, :, 384:512] += jnp.where((lane == 127) & jnp.logical_not(has_right), folded, z)
 
@@ -659,9 +662,9 @@
             vmem((4, 8, 128), jnp.int32), vmem((3, 4, 8, 128), F32), vmem((1040, 256), BF16),
             vmem((GROUP, 2, CAP, 128), F32), vmem((ITERS, GROUP, 2, CAP, 128), F32), vmem((ITERS, GROUP, 2, CAP, 128), F32),
             vmem((528, 512), F32),
-            vmem((2, 8, 128), F32), vmem((ITERS, 4, 8, 128), F32),
-            vmem((ITERS, 2, 8, 640), F32), vmem((8, 640), F32), vmem((ITERS, 4, 8, 128), F32), vmem((2, 8, 128), F32),
-            vmem((ITERS, 2, 8, 256), F32), vmem((2, 8, 128), F32), vmem((8, 256), F32), vmem((8, 128), F32),
+            vmem((2, 8, 128), F32), vmem((ITERS, 4, 8, 128), F32), vmem((ITERS, 8, 640), F32),
+            vmem((ITERS, 8, 640), F32), vmem((8, 640), F32), vmem((ITERS, 4, 8, 128), F32), vmem((2, 8, 128), F32),
+            vmem((ITERS, 8, 256), F32), vmem((8, 128), F32), vmem((8, 256), F32), vmem((8, 128), F32),
             vmem((3, 8, 128), F32), vmem((13, 8, 128), F32),
             dma((1,)),
             dma((GROUP,)), dma((GROUP,)),

time: 48.6 us -> 48.5 us (level)
  no operation moved by 1% of the time
where the time goes in v6:
time: 48.5 us; the launch traced here: 47.9 us
  Pallas kernels  47.2 us (97%)
  between operations  0.65 us (1%)
    pallas_call x1, Pallas kernels, body(): pl.pallas_call(functools.partial(kernel, n_rows, n_cols), out_shape=(tile...  38 us
    pallas_call x1, Pallas kernels, body(): pl.pallas_call(functools.partial(halo_kernel, n_rows, n_cols), out_shape=...  8.38 us

profile of v6, /device:TPU:40, one launch (start us, length us, event | category | flops | bytes accessed | tf_op | source)
XLA Modules:
  0.0 47.9 jit_solution(16490783141864768804)
XLA Ops:
  0.6 8.4 %halos.1 = (f32[2,18,8,640]{3,2,1,0:T(8,128)S(1)}, f32[2,4,8,128]{3,2,1,0:T(8,128)S(1)}, f32[2,4,8,128]{3,2,1,0:T(8,128)S(1)}, f32[12,2,8,128]{3,2,1,0:T(8,128)S...) custom-call(f32[16,8,512]{2,1,0:T(8,128)} %bitcast.8, f32[16,8,512]{2,1,0:T(8,128)} %bitcast.9, f32[2,4096]{1,0:T(2,128)} %off_in.1, ...), custom_call_target="tpu_custom_call" | custom-call | tf_op jit(solution)/shard_map/halos/pallas_call | solution.py:632
  9.0 38.0 %crowd.1 = (f32[16,8,512]{2,1,0:T(8,128)S(1)}, f32[16,8,512]{2,1,0:T(8,128)S(1)}) custom-call(f32[2,18,8,640]{3,2,1,0:T(8,128)S(1)} %get-tuple-element.12.um, f32[2,4,8,128]{3,2,1,0:T(8,128)S(1)} %get-tuple-element.13.off, f32[2,4,8,128]{3,2,1,0:T(8,128)S(1)} %get-tuple-element.14.frac, f32[12,2,8,128]{3,2,1,0:T(8,128)S(1)} %get-tuple-element.15.static_send, ...), custom_call_target="tpu_custom_call" | custom-call | tf_op jit(solution)/shard_map/crowd/pallas_call | solution.py:655
  47.1 0.8 %write_out.1 = (f32[16,8,512]{2,1,0:T(8,128)}, f32[16,8,512]{2,1,0:T(8,128)}) custom-call(f32[16,8,512]{2,1,0:T(8,128)S(1)} %get-tuple-element.18.value, f32[16,8,512]{2,1,0:T(8,128)S(1)} %get-tuple-element.19.density), custom_call_target="tpu_custom_call" | custom-call | tf_op jit(solution)/shard_map/write_out/pallas_call | solution.py:676

commit v7 on v6

--- a/solution.py
+++ b/solution.py
@@ -473,9 +473,9 @@
             send(*x)
         for t in list(range(1, RT - 1)) + [RT + 1]:
             assemble(t)
-        third = grid[0:RT, :, 384:512].reshape(128, 128).T
         fourth = grid[0:RT, :, 512:640].reshape(128, 128).T
-        g_side_r[it, 0] = third[120:128]
+        if full:
+            g_side_r[it, 0] = grid[0:RT, :, 384:512].reshape(128, 128).T[120:128]
         g_side_r[it, 1] = fourth[0:8]
         g_side_r[it, 2] = grid[RT, :, 384:512]
         g_side_r[it, 3] = grid[RT, :, 512:640]
@@ -483,7 +483,8 @@
             first = grid[0:RT, :, 0:128].reshape(128, 128).T
             g_side_l[0] = first[0:8]
             g_side_l[1] = grid[RT, :, 0:128]
-        send(g_side_r.at[it], g_from_l.at[it], (0, 1))
+        sent = pl.ds(0, 4) if full else pl.ds(1, 3)
+        send(g_side_r.at[it, sent], g_from_l.at[it, sent], (0, 1))
         if full:
             send(g_side_l, g_from_r, (0, -1))
         return copies, targets
@@ -501,9 +502,9 @@
                 grid[RT + 1, :, js] = jnp.where(above, g_from_u[it, :, js], z)
         if full:
             grid[RT] += jnp.where(has_down, g_from_d[...], z)
-        right_rows = g_from_r[0] if full else jnp.zeros((8, 128), F32)
-        strip = jnp.concatenate([right_rows, zero_mid, g_from_l[it, 0]], axis=0).T.reshape(RT, 8, 128)
-        grid[0:RT, :, l4] += jnp.where(side_in, strip, z)
+        if full:
+            strip = jnp.concatenate([g_from_r[0], zero_mid, g_from_l[it, 0]], axis=0).T.reshape(RT, 8, 128)
+            grid[0:RT, :, l4] += jnp.where(side_in, strip, z)
         spill = jnp.concatenate([g_from_l[it, 1], jnp.zeros((120, 128), F32)], axis=0).T.reshape(RT, 8, 128)
         grid[0:RT, :, 0:128] += jnp.where(left0, spill, z)
         edge = jnp.where(lane_left, g_from_l[it, 2], z)

time: 48.5 us -> 48.4 us (level)
  no operation moved by 1% of the time
where the time goes in v7:
time: 48.4 us; the launch traced here: 47.8 us
  Pallas kernels  47.2 us (98%)
  between operations  0.65 us (1%)
    pallas_call x1, Pallas kernels, body(): pl.pallas_call(functools.partial(kernel, n_rows, n_cols), out_shape=(tile...  38 us
    pallas_call x1, Pallas kernels, body(): pl.pallas_call(functools.partial(halo_kernel, n_rows, n_cols), out_shape=...  8.38 us

profile of v7, /device:TPU:40, one launch (start us, length us, event | category | flops | bytes accessed | tf_op | source)
XLA Modules:
  0.0 47.8 jit_solution(9947380975696438476)
XLA Ops:
  0.6 8.4 %halos.1 = (f32[2,18,8,640]{3,2,1,0:T(8,128)S(1)}, f32[2,4,8,128]{3,2,1,0:T(8,128)S(1)}, f32[2,4,8,128]{3,2,1,0:T(8,128)S(1)}, f32[12,2,8,128]{3,2,1,0:T(8,128)S...) custom-call(f32[16,8,512]{2,1,0:T(8,128)} %bitcast.8, f32[16,8,512]{2,1,0:T(8,128)} %bitcast.9, f32[2,4096]{1,0:T(2,128)} %off_in.1, ...), custom_call_target="tpu_custom_call" | custom-call | tf_op jit(solution)/shard_map/halos/pallas_call | solution.py:633
  9.0 38.0 %crowd.1 = (f32[16,8,512]{2,1,0:T(8,128)S(1)}, f32[16,8,512]{2,1,0:T(8,128)S(1)}) custom-call(f32[2,18,8,640]{3,2,1,0:T(8,128)S(1)} %get-tuple-element.12.um, f32[2,4,8,128]{3,2,1,0:T(8,128)S(1)} %get-tuple-element.13.off, f32[2,4,8,128]{3,2,1,0:T(8,128)S(1)} %get-tuple-element.14.frac, f32[12,2,8,128]{3,2,1,0:T(8,128)S(1)} %get-tuple-element.15.static_send, ...), custom_call_target="tpu_custom_call" | custom-call | tf_op jit(solution)/shard_map/crowd/pallas_call | solution.py:656
  47.0 0.8 %write_out.1 = (f32[16,8,512]{2,1,0:T(8,128)}, f32[16,8,512]{2,1,0:T(8,128)}) custom-call(f32[16,8,512]{2,1,0:T(8,128)S(1)} %get-tuple-element.18.value, f32[16,8,512]{2,1,0:T(8,128)S(1)} %get-tuple-element.19.density), custom_call_target="tpu_custom_call" | custom-call | tf_op jit(solution)/shard_map/write_out/pallas_call | solution.py:677
